TPU v7x, 16 devices: a whole 2x2x2 slice. The times are simulated.
16 devices in a mesh: replica: 4 (over z, y), model: 4 (over x, core).
Axes of the slice: x: 2, y: 2, z: 2, core: 2. Of those that a mesh axis runs over, the one named last changes fastest.
Arguments:
- x: bfloat16 [512, 2048], P('replica'), parts along dimension 0
- cache_len: int32 [512], P('replica'), parts along dimension 0
- w_query: bfloat16 [2, 2048, 2048], P(None, None, 'model')
- w_key: bfloat16 [2, 2048, 256], replicated
- w_value: bfloat16 [2, 2048, 256], replicated
- w_out: bfloat16 [2, 2048, 2048], P(None, 'model')
- k_cache: bfloat16 [2, 512, 512, 256], P(None, ('replica', 'model')), parts along dimension 1
- v_cache: bfloat16 [2, 512, 512, 256], P(None, ('replica', 'model')), parts along dimension 1
Outputs:
- output 1: bfloat16 [512, 2048], P('replica'), parts along dimension 0
- output 2: bfloat16 [2, 512, 512, 256], P(None, ('replica', 'model')), parts along dimension 1
- output 3: bfloat16 [2, 512, 512, 256], P(None, ('replica', 'model')), parts along dimension 1
There are 4 independent parts. A program takes and returns all parts, laid end to end along the dimension named above; an argument that names none is the same for every part.
All inputs are finite; a program needn't handle non-finite values.
Results may differ from a plain program's by a relative error of at most 0.00437.
Values are sent between devices in bfloat16 or wider.
A program may use at most 1 GiB of HBM per device.

v0:
```python
import jax
import jax.numpy as jnp
from jax import lax
from jax.sharding import PartitionSpec as P, NamedSharding


def write_token(cache, new_rows, cache_len):
    positions = lax.broadcasted_iota(jnp.int32, (1, cache.shape[1], 1), 1)
    return jnp.where(positions == cache_len[:, None, None], new_rows[:, None, :], cache)


def attend_rows(query, k_layer, v_layer, cache_len):
    seq_len = k_layer.shape[1]
    head_dim = k_layer.shape[2]
    scores = jnp.einsum("bhd,bsd->bhs", query, k_layer, preferred_element_type=jnp.float32) * (head_dim ** -0.5)
    positions = lax.broadcasted_iota(jnp.int32, (1, 1, seq_len), 2)
    scores = jnp.where(positions <= cache_len[:, None, None], scores, -jnp.inf)
    weights = jax.nn.softmax(scores, axis=-1).astype(jnp.bfloat16)
    context = jnp.einsum("bhs,bsd->bhd", weights, v_layer, preferred_element_type=jnp.float32)
    return context.astype(jnp.bfloat16)


def solution(mesh):
    groups = mesh.shape["model"]
    row_axes = ("replica", "model")
    cache_spec = P(None, row_axes, None, None)

    def device_step(x, cache_len, w_query, w_key, w_value, w_out, k_cache, v_cache):
        rows = x.shape[0]
        local_rows = rows // groups
        head_dim = k_cache.shape[-1]
        local_heads = w_query.shape[-1] // head_dim
        first_row = lax.axis_index("model") * local_rows
        my_len = lax.dynamic_slice_in_dim(cache_len, first_row, local_rows)
        hidden = x
        k_layers = []
        v_layers = []
        for layer in range(w_query.shape[0]):
            my_rows = lax.dynamic_slice_in_dim(hidden, first_row, local_rows)
            query = jnp.dot(hidden, w_query[layer], preferred_element_type=jnp.float32).astype(jnp.bfloat16)
            query = query.reshape(rows, local_heads, head_dim)
            k_new = jnp.dot(my_rows, w_key[layer], preferred_element_type=jnp.float32).astype(jnp.bfloat16)
            v_new = jnp.dot(my_rows, w_value[layer], preferred_element_type=jnp.float32).astype(jnp.bfloat16)
            k_layer = write_token(k_cache[layer], k_new, my_len)
            v_layer = write_token(v_cache[layer], v_new, my_len)
            query = lax.all_to_all(query, "model", 0, 1, tiled=True)
            context = attend_rows(query, k_layer, v_layer, my_len)
            context = lax.all_to_all(context, "model", 1, 0, tiled=True)
            part_sum = jnp.dot(context.reshape(rows, local_heads * head_dim), w_out[layer], preferred_element_type=jnp.float32)
            total = lax.psum(part_sum, "model")
            hidden = (hidden.astype(jnp.float32) + total).astype(jnp.bfloat16)
            k_layers.append(k_layer)
            v_layers.append(v_layer)
        return hidden, jnp.stack(k_layers), jnp.stack(v_layers)

    return jax.shard_map(
        device_step,
        mesh=mesh,
        in_specs=(P("replica", None), P("replica"), P(None, None, "model"), P(), P(), P(None, "model", None), cache_spec, cache_spec),
        out_specs=(P("replica", None), cache_spec, cache_spec),
        check_vma=False,
    )
```

profile of v0, /device:TPU:0, one launch (start us, length us, event | category | flops | bytes accessed | tf_op | source)
XLA Modules:
  0.0 174.0 jit_solution(13482329788446382763)
XLA Ops:
  7.2 2.2 %fusion.38 = bf16[128,512]{1,0:T(8,128)(2,1)S(1)} fusion(bf16[128,2048]{1,0:T(8,128)(2,1)} %param.8, bf16[2,2048,512]{2,1,0:T(8,128)(2,1)} %param.10), kind=kOutput, calls=%fused_computation.48 | convolution fusion | flops 268500992 | bytes 2752512 | tf_op jit(solution)/shard_map/dot_general | solution.py:40
  10.1 4.5 %all-to-all-start = ((bf16[128,2,256]{2,1,0:T(2,128)(2,1)}), bf16[128,2,256]{2,1,0:T(2,128)(2,1)S(1)}, u32[]{:S(2)}, u32[]{:S(2)}) async-start(bf16[128,2,256]{2,1,0:T(2,128)(2,1)} %reshape.73), calls=%async_computation | async-start | bytes 262144 | tf_op jit(solution)/shard_map/all_to_all | solution.py:46
  14.6 0.7 dynamic_slice.9
  15.3 1.6 convolution_convert_fusion.3
  16.9 1.6 convolution_convert_fusion.2
  19.1 6.6 %fusion.64 = (f32[32,8]{1,0:T(8,128)S(1)}, f32[32,8,512]{2,1,0:T(8,128)}) fusion(bf16[32,8,256]{2,1,0:T(8,128)(2,1)S(1)} %all_to_all.51, pred[32,512]{1,0:T(8,128)(4,1)S(1)} %get-tuple-element.10, bf16[2,32,512,256]{3,2,1,0:T(8,128)(2,1)} %param.14, bf16[32,256]{1,0:T(8,128)(2,1)S(1)} %convolution_convert_fusion.3, pred[32,512]{1,0:T(8,128)(4,1)S(1)} %get-tuple-element.9), kind=kOutput, calls=%fused_computation.82 | convolution fusion | flops 71827968 | bytes 9094144 | tf_op jit(solution)/shard_map/sub | solution.py:18
  25.8 6.5 %fusion.44 = bf16[32,8,256]{2,1,0:T(8,128)(2,1)S(1)} fusion(pred[32,512]{1,0:T(8,128)(4,1)S(1)} %get-tuple-element.10, bf16[2,32,512,256]{3,2,1,0:T(8,128)(2,1)} %param.15, bf16[32,256]{1,0:T(8,128)(2,1)S(1)} %convolution_convert_fusion.2, f32[32,8,512]{2,1,0:T(8,128)} %get-tuple-element.12, f32[32,8]{1,0:T(8,128)S(1)} %get-tuple-element.11), kind=kOutput, calls=%fused_computation.50 | convolution fusion | flops 71630848 | bytes 9077760 | tf_op jit(solution)/shard_map/bhs,bsd->bhd/dot_general | solution.py:19
  32.3 7.4 %all_to_all.66 = bf16[32,8,256]{2,0,1:T(8,128)(2,1)S(1)} all-to-all(bf16[32,8,256]{2,0,1:T(8,128)(2,1)S(1)} %copy.18), channel_id=1, replica_groups=mesh['replica'=4,'model'=4] {'model'}, dimensions={1} | all-to-all | bytes 262144 | tf_op jit(solution)/shard_map/all_to_all | solution.py:48
  39.9 1.4 fusion.22
  41.4 33.4 %all-reduce.3.cloned.1.call-done = f32[128,2048]{1,0:T(8,128)} async-done(((f32[128,2048]{1,0:T(8,128)}), f32[128,2048]{1,0:T(8,128)}) %all-reduce.3.cloned.1.call-update) | async-done | bytes 1048592 | tf_op jit(solution)/shard_map/psum | solution.py:50
  74.8 1.3 add_convert_fusion.1
  76.4 2.0 %fusion.41 = bf16[128,512]{1,0:T(8,128)(2,1)S(1)} fusion(bf16[128,2048]{1,0:T(8,128)(2,1)S(1)} %add_convert_fusion.1, bf16[2,2048,512]{2,1,0:T(8,128)(2,1)} %param.10), kind=kOutput, calls=%fused_computation.49 | convolution fusion | flops 268500992 | bytes 2752512 | tf_op jit(solution)/shard_map/dot_general | solution.py:40
  78.5 0.7 reshape.75
  79.2 3.3 %all-to-all-start.2 = ((bf16[128,2,256]{2,1,0:T(2,128)(2,1)}), bf16[128,2,256]{2,1,0:T(2,128)(2,1)S(1)}, u32[]{:S(2)}, u32[]{:S(2)}) async-start(bf16[128,2,256]{2,1,0:T(2,128)(2,1)} %reshape.75), calls=%async_computation.2 | async-start | bytes 262144 | tf_op jit(solution)/shard_map/all_to_all | solution.py:46
  82.5 1.5 convolution_convert_fusion.1
  84.0 2.8 %all-to-all-done.2 = bf16[128,2,256]{2,1,0:T(2,128)(2,1)S(1)} async-done(((bf16[128,2,256]{2,1,0:T(2,128)(2,1)}), bf16[128,2,256]{2,1,0:T(2,128)(2,1)S(1)}, u32[]{:S(2)}, u32[]{:S(2)}) %all-to-all-start.2) | async-done | bytes 131104 | tf_op jit(solution)/shard_map/all_to_all | solution.py:46
  87.0 8.3 %fusion.65 = (f32[32,8]{1,0:T(8,128)S(1)}, f32[32,8,512]{2,1,0:T(8,128)S(1)}) fusion(bf16[32,8,256]{2,1,0:T(8,128)(2,1)S(1)} %all_to_all.58, pred[32,512]{1,0:T(8,128)(4,1)S(1)} %get-tuple-element.10, bf16[2,32,512,256]{3,2,1,0:T(8,128)(2,1)} %param.14, bf16[32,256]{1,0:T(8,128)(2,1)S(1)} %convolution_convert_fusion.1, pred[32,512]{1,0:T(8,128)(4,1)S(1)} %get-tuple-element.9), kind=kOutput, calls=%fused_computation.83 | convolution fusion | flops 71827968 | bytes 9094144 | tf_op jit(solution)/shard_map/sub | solution.py:18
  95.3 5.6 %fusion.45 = bf16[32,8,256]{2,1,0:T(8,128)(2,1)S(1)} fusion(pred[32,512]{1,0:T(8,128)(4,1)S(1)} %get-tuple-element.10, bf16[2,32,512,256]{3,2,1,0:T(8,128)(2,1)} %param.15, bf16[32,256]{1,0:T(8,128)(2,1)S(1)} %convolution_convert_fusion, f32[32,8,512]{2,1,0:T(8,128)S(1)} %get-tuple-element.14, f32[32,8]{1,0:T(8,128)S(1)} %get-tuple-element.13), kind=kOutput, calls=%fused_computation.51 | convolution fusion | flops 71630848 | bytes 9077760 | tf_op jit(solution)/shard_map/bhs,bsd->bhd/dot_general | solution.py:19
  101.6 3.3 %all-to-all-start.3 = ((bf16[32,8,256]{2,0,1:T(8,128)(2,1)}), bf16[32,8,256]{2,0,1:T(8,128)(2,1)S(1)}, u32[]{:S(2)}, u32[]{:S(2)}) async-start(bf16[32,8,256]{2,0,1:T(8,128)(2,1)} %copy.21), calls=%async_computation.3 | async-start | bytes 262144 | tf_op jit(solution)/shard_map/all_to_all | solution.py:48
  104.9 22.7 %broadcast_select_fusion.1 = (bf16[1,32,512,256]{3,2,1,0:T(8,128)(2,1)}, bf16[1,32,512,256]{3,2,1,0:T(8,128)(2,1)}, bf16[1,32,512,256]{3,2,1,0:T(8,128)(2,1)}, bf16[1,32,512,256]{3,2,1,0:T(8,128)(2,1)}) fusion(pred[32,512]{1,0:T(8,128)(4,1)S(1)} %get-tuple-element.10, bf16[2,32,512,256]{3,2,1,0:T(8,128)(2,1)} %param.15, ...), kind=kLoop, calls=%fused_computation.13 | loop fusion | flops 16777216 | bytes 67190784 | tf_op jit(solution)/shard_map/jit(_where)/select_n | solution.py:9
  127.8 3.0 %fusion.18 = f32[128,2048]{1,0:T(8,128)} fusion(bf16[128,512]{1,0:T(8,128)(2,1)S(1)} %bitcast.81, bf16[2,512,2048]{2,1,0:T(8,128)(2,1)} %param.13), kind=kOutput, calls=%fused_computation.28 | convolution fusion | flops 268435456 | bytes 3276800 | tf_op jit(solution)/shard_map/dot_general | solution.py:49
  130.8 22.8 %pad_maximum_fusion = (bf16[2,32,512,256]{3,2,1,0:T(8,128)(2,1)}, bf16[2,32,512,256]{3,2,1,0:T(8,128)(2,1)}) fusion(bf16[1,32,512,256]{3,2,1,0:T(8,128)(2,1)} %get-tuple-element.7, bf16[1,32,512,256]{3,2,1,0:T(8,128)(2,1)} %get-tuple-element.8, bf16[1,32,512,256]{3,2,1,0:T(8,128)(2,1)} %get-tuple-element.4, bf16[1,32,512,256]{3,2,1,0:T(8,128)(2,1)} %get-tuple-element.3), kind=kLoop, calls=%fused_computation.2 | loop fusion | flops 16777216 | bytes 67108864 | tf_op jit(solution)/shard_map/stack | solution.py:54
  153.6 11.4 %all-reduce.5.cloned.1.call-done = f32[128,2048]{1,0:T(8,128)} async-done(((f32[128,2048]{1,0:T(8,128)}), f32[128,2048]{1,0:T(8,128)}) %all-reduce.5.cloned.1.call-update) | async-done | bytes 1048592 | tf_op jit(solution)/shard_map/psum | solution.py:50
  165.0 2.1 %add_convert_fusion = bf16[128,2048]{1,0:T(8,128)(2,1)} fusion(f32[128,2048]{1,0:T(8,128)} %all-reduce.5.cloned.1.call-done, bf16[128,2048]{1,0:T(8,128)(2,1)S(1)} %add_convert_fusion.1), kind=kLoop, calls=%fused_computation.60 | loop fusion | flops 786432 | bytes 2097152 | tf_op jit(solution)/shard_map/convert_element_type | solution.py:51
  (25 shorter events, 2.9 us)
Async XLA Ops:
  10.1 8.9 %all-to-all-start = ((bf16[128,2,256]{2,1,0:T(2,128)(2,1)}), bf16[128,2,256]{2,1,0:T(2,128)(2,1)S(1)}, u32[]{:S(2)}, u32[]{:S(2)}) async-start(bf16[128,2,256]{2,1,0:T(2,128)(2,1)} %reshape.73), calls=%async_computation | async-start | bytes 262144 | tf_op jit(solution)/shard_map/all_to_all | solution.py:46
  14.6 60.2 %all-reduce.3.cloned.1.call-start = ((), (), s32[]{:S(2)}) async-start(), calls=%async_computation.4 | async-start | bytes 2097152 | tf_op jit(solution)/shard_map/psum | solution.py:50
  25.8 14.1 %copy-start = (bf16[2,512,2048]{2,1,0:T(8,128)(2,1)S(1)}, bf16[2,512,2048]{2,1,0:T(8,128)(2,1)}, u32[]{:S(2)}) copy-start(bf16[2,512,2048]{2,1,0:T(8,128)(2,1)} %param.13) | copy-start | bytes 12582916
  25.8 49.0 %copy-start.1 = (bf16[128,2048]{1,0:T(8,128)(2,1)S(1)}, bf16[128,2048]{1,0:T(8,128)(2,1)}, u32[]{:S(2)}) copy-start(bf16[128,2048]{1,0:T(8,128)(2,1)} %param.8) | copy-start | bytes 1572868
  25.8 50.3 %copy-start.2 = (bf16[2,2048,256]{2,1,0:T(8,128)(2,1)S(1)}, bf16[2,2048,256]{2,1,0:T(8,128)(2,1)}, u32[]{:S(2)}) copy-start(bf16[2,2048,256]{2,1,0:T(8,128)(2,1)} %param.12) | copy-start | bytes 6291460
  79.2 7.7 %all-to-all-start.2 = ((bf16[128,2,256]{2,1,0:T(2,128)(2,1)}), bf16[128,2,256]{2,1,0:T(2,128)(2,1)S(1)}, u32[]{:S(2)}, u32[]{:S(2)}) async-start(bf16[128,2,256]{2,1,0:T(2,128)(2,1)} %reshape.75), calls=%async_computation.2 | async-start | bytes 262144 | tf_op jit(solution)/shard_map/all_to_all | solution.py:46
  101.6 26.1 %all-to-all-start.3 = ((bf16[32,8,256]{2,0,1:T(8,128)(2,1)}), bf16[32,8,256]{2,0,1:T(8,128)(2,1)S(1)}, u32[]{:S(2)}, u32[]{:S(2)}) async-start(bf16[32,8,256]{2,0,1:T(8,128)(2,1)} %copy.21), calls=%async_computation.3 | async-start | bytes 262144 | tf_op jit(solution)/shard_map/all_to_all | solution.py:48
  104.9 60.1 %all-reduce.5.cloned.1.call-start = ((), (), s32[]{:S(2)}) async-start(), calls=%async_computation.5 | async-start | bytes 2097152 | tf_op jit(solution)/shard_map/psum | solution.py:50
Sparse Core Ops, SparseCore 0:
  41.5 33.2 all-reduce.2
  131.0 34.0 all-reduce.4
where the time goes:
time: 175 us; the launch traced here: 174 us
  other arithmetic  49 us (28%)
  waiting for transfers between devices  48.1 us (27%)
  matrix products  40.7 us (23%)
  between operations  14.2 us (8%)
  starting transfers between devices  11.2 us (6%)
  blocking collectives  7.41 us (4%)
  local copies, waits for them, and re-layouts  3.45 us (2%)
    psum x2, waiting for transfers between devices, device_step(): total = lax.psum(part_sum, 'model')  44.8 us
    another operation x1, other arithmetic, device_step(): return (hidden, jnp.stack(k_layers), jnp.stack(v_layers))  22.8 us
    select_n x1, other arithmetic, write_token(): jnp.where(positions == cache_len[:, None, None], new_rows[:, None, :], ca...  22.7 us
    sub x2, matrix products, attend_rows(): weights = jax.nn.softmax(scores, axis=-1).astype(jnp.bfloat16)  14.9 us
    dot_general x2, matrix products, attend_rows(): jnp.einsum('bhs,bsd->bhd', weights, v_layer, preferred_element_type=jnp.f...  12.1 us
    all_to_all x2, starting transfers between devices, device_step(): query = lax.all_to_all(query, 'model', 0, 1, tiled=True)  7.82 us
    all_to_all x1, blocking collectives, device_step(): context = lax.all_to_all(context, 'model', 1, 0, tiled=True)  7.41 us
    dot_general x2, matrix products, device_step(): jnp.dot(context.reshape(rows, local_heads * head_dim), w_out[layer], pref...  4.48 us
  transfers between devices with their start and end apart: 5, of which 4 were waited for; matrix products, arithmetic and copies ran while one was open for 29% of the time, Pallas kernels for 0%

commit v1 on v0

v1 whole, which is shorter than its diff:
```python
import functools

import jax
import jax.numpy as jnp
from jax import lax
from jax.experimental import pallas as pl
from jax.experimental.pallas import tpu as pltpu
from jax.sharding import PartitionSpec as P

F32 = jnp.float32
BF16 = jnp.bfloat16
MESH = pl.DeviceIdType.MESH
HBM = pl.BlockSpec(memory_space=pltpu.HBM)
VM = pl.BlockSpec(memory_space=pltpu.VMEM)
SM = pl.BlockSpec(memory_space=pltpu.SMEM)
DMA = pltpu.SemaphoreType.DMA


def dot(a, b):
    return jnp.dot(a, b, preferred_element_type=F32)


def place():
    m = lax.axis_index("model")
    return lax.axis_index("replica"), m, lax.rem(m, 2), m // 2


def meet(peers):
    barrier = pltpu.get_barrier_semaphore()
    for peer in peers:
        pl.semaphore_signal(barrier, inc=1, device_id=peer, device_id_type=MESH)
    pl.semaphore_wait(barrier, len(peers))


def send(src, dst, send_sem, recv_sem, peer):
    return pltpu.make_async_remote_copy(
        src_ref=src, dst_ref=dst, send_sem=send_sem, recv_sem=recv_sem, device_id=peer, device_id_type=MESH)


def first_kernel(x_hbm, wq_hbm, wk_hbm, wv_hbm, kc_hbm, vc_hbm,
                 q_out, kn_out, vn_out, kb, vb,
                 xs, wqs, wks, wvs, qown, qrecv,
                 wsem, csem, qsend, qrecv_sem):
    rep, m, core, chip = place()
    rows = q_out.shape[1]
    across, diag, mate = (rep, lax.rem(m + 2, 4)), (rep, 3 - m), (rep, m + 1 - 2 * core)
    loads = [pltpu.make_async_copy(x_hbm, xs, wsem.at[0])]
    for i in range(2):
        loads.append(pltpu.make_async_copy(wq_hbm.at[0, :, pl.ds(i * 256, 256)], wqs.at[i], wsem.at[1 + i]))
    loads.append(pltpu.make_async_copy(wk_hbm.at[0], wks, wsem.at[3]))
    loads.append(pltpu.make_async_copy(wv_hbm.at[0], wvs, wsem.at[4]))
    for load in loads:
        load.start()
    caches = [pltpu.make_async_copy(kc_hbm.at[0], kb, csem.at[0]), pltpu.make_async_copy(vc_hbm.at[0], vb, csem.at[1])]
    meet((across, diag, mate))
    loads[0].wait()
    copies = []
    for i in range(2):
        loads[1 + i].wait()
        if i == 1:
            for c in caches:
                c.start()
        q = dot(xs[...], wqs[i]).astype(BF16)
        for d in range(4):
            qown[d, i] = q[d * rows:(d + 1) * rows]
        for n, (peer, who) in enumerate(((across, lax.rem(m + 2, 4)), (diag, 3 - m), (mate, m + 1 - 2 * core))):
            c = send(qown.at[who, i], qrecv.at[m, i], qsend.at[n, i], qrecv_sem.at[n, i], peer)
            c.start()
            copies.append(c)
        qrecv[m, i] = qown[m, i]
    mine = xs[pl.ds(pl.multiple_of(m * rows, rows), rows), :]
    loads[3].wait()
    kn_out[...] = dot(mine, wks[...]).astype(BF16).astype(F32)
    loads[4].wait()
    vn_out[...] = dot(mine, wvs[...]).astype(BF16).astype(F32)
    for c in copies:
        c.wait()
    for s in range(4):
        for i in range(2):
            q_out[2 * s + i] = qrecv[s, i]
    for c in caches:
        c.wait()


def attend_kernel(*refs, layer):
    if layer:
        len_ref, q_ref, kn, vn, kb, vb, _, _, ctx, _, _, ko, vo, qs, st, acc, osem = refs
    else:
        len_ref, q_ref, kn, vn, kb, vb, ctx, _, _, ko, vo, qs, st, acc, osem = refs
    heads, rows, dim = q_ref.shape
    seq = kb.shape[1]
    base = lax.axis_index("model") * rows
    half = 16

    def patch(b, carry):
        ln = len_ref[base + b]
        start = pl.multiple_of((ln // half) * half, half)
        hit = lax.broadcasted_iota(jnp.int32, (half, dim), 0) == ln - start
        for buf, new in ((kb, kn), (vb, vn)):
            old = buf[b, pl.ds(start, half), :].astype(F32)
            buf[b, pl.ds(start, half), :] = jnp.where(hit, new[pl.ds(b, 1), :], old).astype(BF16)
        return carry

    lax.fori_loop(0, rows, patch, 0, unroll=4)
    outs = []
    step = 4
    for i in range(rows // step):
        for n, (src, dst) in enumerate(((kb, ko), (vb, vo))):
            c = pltpu.make_async_copy(src.at[pl.ds(i * step, step)], dst.at[layer, pl.ds(i * step, step)], osem.at[n, i])
            c.start()
            outs.append(c)
    lanes = heads * half
    lane_b = lax.rem(lax.broadcasted_iota(jnp.int32, (1, lanes), 1), half)
    row_b = lax.rem(lax.broadcasted_iota(jnp.int32, (lanes, 1), 0), half)
    pos = lax.broadcasted_iota(jnp.int32, (seq, lanes), 0)
    for g in range(rows // half):
        for h in range(heads):
            qs[h * half:(h + 1) * half, :] = q_ref[h, g * half:(g + 1) * half, :]
        lens = jnp.zeros((1, lanes), jnp.int32)
        for b in range(half):
            lens = jnp.where(lane_b == b, len_ref[base + g * half + b], lens)

        def scores(b, carry):
            s = lax.dot_general(kb[g * half + b], qs[...], (((1,), (1,)), ((), ())), preferred_element_type=F32)
            st[...] = jnp.where(lane_b == b, s, st[...])
            return carry

        lax.fori_loop(0, half, scores, 0, unroll=2)
        s = jnp.where(pos <= lens, st[...] * (dim ** -0.5), -jnp.inf)
        e = jnp.exp(s - jnp.max(s, axis=0, keepdims=True))
        p = e * (1.0 / jnp.sum(e, axis=0, keepdims=True))
        p = p.T.astype(BF16)

        def mix(b, carry):
            c = dot(p, vb[g * half + b])
            acc[...] = jnp.where(row_b == b, c, acc[...])
            return carry

        lax.fori_loop(0, half, mix, 0, unroll=2)
        for h in range(heads):
            ctx[h, g * half:(g + 1) * half, :] = acc[h * half:(h + 1) * half, :].astype(BF16)
    for c in outs:
        c.wait()


def exchange_kernel(*refs, layer, last):
    if last:
        (ctx, hid, wo_hbm, out,
         wos, lhs, ys, yrecv, hl, pown, pfwd,
         wsem, csem, ysem, hsem, psem, fsem) = refs
    else:
        (ctx, x_hbm, wo_hbm, wq_hbm, wk_hbm, wv_hbm, kc_hbm, vc_hbm,
         q_out, kn_out, vn_out, hid_out, kb, vb,
         wos, lhs, ys, yrecv, hl, xs, wqs, wks, wvs, qacc, qown, qrecv,
         wsem, csem, ysem, hsem, qsem, kvsem) = refs
    rep, m, core, chip = place()
    across_m, mate_m = lax.rem(m + 2, 4), m + 1 - 2 * core
    across, mate = (rep, across_m), (rep, mate_m)
    rows = ctx.shape[1]
    chunks = hl.shape[0]
    load_wo = pltpu.make_async_copy(wo_hbm.at[layer], wos.at[core], wsem.at[0])
    load_wo.start()
    if not last:
        load_x = pltpu.make_async_copy(x_hbm.at[pl.ds(pl.multiple_of(m * rows, rows), rows)], xs, wsem.at[1])
        load_q = pltpu.make_async_copy(wq_hbm.at[layer + 1], wqs.at[core], wsem.at[2])
        load_k = pltpu.make_async_copy(wk_hbm.at[layer + 1], wks, wsem.at[3])
        load_v = pltpu.make_async_copy(wv_hbm.at[layer + 1], wvs, wsem.at[4])
        for c in (load_x, load_q, load_k, load_v):
            c.start()
    meet((across, mate))
    give = send(ctx.at[pl.ds((1 - chip) * 4, 4)], lhs.at[:, pl.ds(rows, rows), :], csem.at[0], csem.at[1], across)
    give.start()
    load_wo.wait()
    push_wo = send(wos.at[core], wos.at[core], wsem.at[5], wsem.at[6], mate)
    push_wo.start()
    if not last:
        load_q.wait()
        push_q = send(wqs.at[core], wqs.at[core], wsem.at[7], wsem.at[8], mate)
        push_q.start()
        caches = [pltpu.make_async_copy(kc_hbm.at[layer + 1], kb, kvsem.at[0]),
                  pltpu.make_async_copy(vc_hbm.at[layer + 1], vb, kvsem.at[1])]
        for c in caches:
            c.start()
    for i in range(4):
        lhs[i, 0:rows, :] = ctx[chip * 4 + i]
    give.wait()
    push_wo.wait()
    ycopies = []
    for j in range(chunks):
        y = dot(lhs[0], wos[0, 0:256, j * 256:(j + 1) * 256])
        for i in range(1, 4):
            y += dot(lhs[i], wos[i // 2, (i % 2) * 256:(i % 2 + 1) * 256, j * 256:(j + 1) * 256])
        ys[j] = y
        c = send(ys.at[j, pl.ds(rows, rows)], yrecv.at[j], ysem.at[0, j], ysem.at[1, j], across)
        c.start()
        ycopies.append(c)
    if not last:
        load_x.wait()
    hcopies = []
    pcopies = []
    for j in range(chunks):
        ycopies[j].wait_recv()
        old = hid[j] if last else xs[:, j * 256:(j + 1) * 256]
        new = (old.astype(F32) + (ys[j, 0:rows, :] + yrecv[j])).astype(BF16)
        hl[j, 0:rows, :] = new
        c = send(hl.at[j, pl.ds(0, rows)], hl.at[j, pl.ds(rows, rows)], hsem.at[0, j], hsem.at[1, j], across)
        c.start()
        hcopies.append(c)
        if last:
            c = send(hl.at[j, pl.ds(0, rows)], pown.at[j], psem.at[0, j], psem.at[1, j], mate)
            c.start()
            pcopies.append(c)
    if last:
        fcopies = []
        for j in range(chunks):
            hcopies[j].wait_recv()
            c = send(hl.at[j, pl.ds(rows, rows)], pfwd.at[j], fsem.at[0, j], fsem.at[1, j], mate)
            c.start()
            fcopies.append(c)
        for j in range(chunks):
            cols = slice(j * 256, (j + 1) * 256)
            out[pl.ds(pl.multiple_of(m * rows, rows), rows), cols] = hl[j, 0:rows, :]
            out[pl.ds(pl.multiple_of(across_m * rows, rows), rows), cols] = hl[j, rows:2 * rows, :]
        for j in range(chunks):
            cols = slice(j * 256, (j + 1) * 256)
            pcopies[j].wait_recv()
            out[pl.ds(pl.multiple_of(mate_m * rows, rows), rows), cols] = pown[j]
            fcopies[j].wait_recv()
            out[pl.ds(pl.multiple_of((3 - m) * rows, rows), rows), cols] = pfwd[j]
        for c in ycopies + hcopies + pcopies + fcopies:
            c.wait_send()
        return
    push_q.wait()
    for j in range(chunks):
        hcopies[j].wait_recv()
        for i in range(4):
            part = dot(hl[j], wqs[i // 2, j * 256:(j + 1) * 256, (i % 2) * 256:(i % 2 + 1) * 256])
            if j == 0:
                qacc[i] = part
            else:
                qacc[i] += part
    qcopies = []
    for i in range(4):
        qown[i] = qacc[i].astype(BF16)
        c = send(qown.at[i, pl.ds(rows, rows)], qrecv.at[i], qsem.at[0, i], qsem.at[1, i], across)
        c.start()
        qcopies.append(c)
    for load, w, res in ((load_k, wks, kn_out), (load_v, wvs, vn_out)):
        load.wait()
        t = dot(hl[0, 0:rows, :], w[0:256, :])
        for j in range(1, chunks):
            t += dot(hl[j, 0:rows, :], w[j * 256:(j + 1) * 256, :])
        res[...] = t.astype(BF16).astype(F32)
    for j in range(chunks):
        hid_out[j] = hl[j, 0:rows, :]
    for i in range(4):
        q_out[chip * 4 + i] = qown[i, 0:rows, :]
    for i in range(4):
        qcopies[i].wait_recv()
        q_out[(1 - chip) * 4 + i] = qrecv[i]
    for c in ycopies + hcopies + qcopies:
        c.wait_send()
    for c in caches:
        c.wait()


def solution(mesh):
    groups = mesh.shape["model"]
    row_axes = ("replica", "model")
    cache_spec = P(None, row_axes, None, None)

    def device_step(x, cache_len, w_query, w_key, w_value, w_out, k_cache, v_cache):
        layers, rows, seq, dim = k_cache.shape
        total, width = x.shape
        chunks = width // dim
        heads = w_query.shape[-1] // dim * groups
        local = w_query.shape[-1]
        hd = (heads, rows, dim)
        x, w_query, w_key, w_value, w_out, k_cache, v_cache = (
            pltpu.with_memory_space_constraint(a, pltpu.HBM)
            for a in (x, w_query, w_key, w_value, w_out, k_cache, v_cache))
        remote = functools.partial(pltpu.CompilerParams, has_side_effects=True)

        q, kn, vn, kb, vb = pl.pallas_call(
            first_kernel,
            out_shape=(pltpu.VMEM(hd, BF16), pltpu.VMEM((rows, dim), F32), pltpu.VMEM((rows, dim), F32),
                       pltpu.VMEM((rows, seq, dim), BF16), pltpu.VMEM((rows, seq, dim), BF16)),
            in_specs=[HBM] * 6,
            out_specs=(VM,) * 5,
            scratch_shapes=[
                pltpu.VMEM((total, width), BF16), pltpu.VMEM((2, width, dim), BF16),
                pltpu.VMEM((width, dim), BF16), pltpu.VMEM((width, dim), BF16),
                pltpu.VMEM((4, 2, rows, dim), BF16), pltpu.VMEM((4, 2, rows, dim), BF16),
                DMA((5,)), DMA((2,)), DMA((3, 2)), DMA((3, 2)),
            ],
            compiler_params=remote(collective_id=0, vmem_limit_bytes=16 << 20),
            name="first",
        )(x, w_query, w_key, w_value, k_cache, v_cache)

        ko = vo = None
        hid = x
        for layer in range(layers):
            last = layer == layers - 1
            ins = (cache_len, q, kn, vn, kb, vb) + ((ko, vo) if layer else ())
            ctx, _, _, ko, vo = pl.pallas_call(
                functools.partial(attend_kernel, layer=layer),
                out_shape=(pltpu.VMEM(hd, BF16), pltpu.VMEM(kb.shape, BF16), pltpu.VMEM(vb.shape, BF16),
                           jax.ShapeDtypeStruct(k_cache.shape, BF16), jax.ShapeDtypeStruct(v_cache.shape, BF16)),
                in_specs=[SM] + [VM] * 5 + ([HBM, HBM] if layer else []),
                out_specs=(VM, VM, VM, HBM, HBM),
                input_output_aliases={4: 1, 5: 2, 6: 3, 7: 4} if layer else {4: 1, 5: 2},
                scratch_shapes=[
                    pltpu.VMEM((heads * 16, dim), BF16), pltpu.VMEM((seq, heads * 16), F32),
                    pltpu.VMEM((heads * 16, dim), F32), DMA((2, rows // 4)),
                ],
                compiler_params=pltpu.CompilerParams(vmem_limit_bytes=8 << 20),
                name=f"attend{layer}",
            )(*ins)
            common = [
                pltpu.VMEM((2, local, width), BF16), pltpu.VMEM((4, 2 * rows, dim), BF16),
                pltpu.VMEM((chunks, 2 * rows, dim), F32), pltpu.VMEM((chunks, rows, dim), F32),
                pltpu.VMEM((chunks, 2 * rows, dim), BF16),
            ]
            sems = [DMA((9,)), DMA((2,)), DMA((2, chunks)), DMA((2, chunks))]
            if last:
                out = pl.pallas_call(
                    functools.partial(exchange_kernel, layer=layer, last=True),
                    out_shape=pltpu.VMEM((total, width), BF16),
                    in_specs=[VM, VM, HBM],
                    out_specs=VM,
                    scratch_shapes=common + [pltpu.VMEM((chunks, rows, dim), BF16)] * 2
                    + sems + [DMA((2, chunks)), DMA((2, chunks))],
                    compiler_params=remote(collective_id=layer + 1, vmem_limit_bytes=16 << 20),
                    name="last",
                )(ctx, hid, w_out)
            else:
                q, kn, vn, hid, kb, vb = pl.pallas_call(
                    functools.partial(exchange_kernel, layer=layer, last=False),
                    out_shape=(pltpu.VMEM(hd, BF16), pltpu.VMEM((rows, dim), F32), pltpu.VMEM((rows, dim), F32),
                               pltpu.VMEM((chunks, rows, dim), BF16),
                               pltpu.VMEM((rows, seq, dim), BF16), pltpu.VMEM((rows, seq, dim), BF16)),
                    in_specs=[VM] + [HBM] * 7,
                    out_specs=(VM,) * 6,
                    scratch_shapes=common + [
                        pltpu.VMEM((rows, width), BF16), pltpu.VMEM((2, width, local), BF16),
                        pltpu.VMEM((width, dim), BF16), pltpu.VMEM((width, dim), BF16),
                        pltpu.VMEM((4, 2 * rows, dim), F32), pltpu.VMEM((4, 2 * rows, dim), BF16),
                        pltpu.VMEM((4, rows, dim), BF16),
                    ] + sems + [DMA((2, 4)), DMA((2,))],
                    compiler_params=remote(collective_id=layer + 1, vmem_limit_bytes=24 << 20),
                    name="middle",
                )(ctx, hid, w_out, w_query, w_key, w_value, k_cache, v_cache)
        return out, ko, vo

    return jax.shard_map(
        device_step,
        mesh=mesh,
        in_specs=(P("replica", None), P("replica"), P(None, None, "model"), P(), P(), P(None, "model", None), cache_spec, cache_spec),
        out_specs=(P("replica", None), cache_spec, cache_spec),
        check_vma=False,
    )
```

time: 175 us -> 70.6 us (0.40)
  Pallas kernels: 0 us -> 69 us
  other arithmetic: 49 us -> 0 us
  waiting for transfers between devices: 48.1 us -> 0 us
  matrix products: 40.7 us -> 0 us
  between operations: 14.2 us -> 0.69 us
  starting transfers between devices: 11.2 us -> 0 us
  blocking collectives: 7.41 us -> 0 us
  local copies, waits for them, and re-layouts: 3.45 us -> 0.8 us
    pallas_call x0 -> x5, Pallas kernels: none -> 69 us  [the longest x1 21 us: device_step(): pl.pallas_call(functools.partial(exchange_kernel, layer=layer, last=False...]
    psum x2 -> x0, waiting for transfers between devices: 44.8 us -> none  [device_step(): total = lax.psum(part_sum, 'model')]
    dot_general x10 -> x0, matrix products: 25.8 us -> none  [the longest x2 12.1 us: attend_rows(): jnp.einsum('bhs,bsd->bhd', weights, v_layer, preferred_element_type=jnp.f...]
    another operation x1 -> x0, other arithmetic: 22.8 us -> none  [device_step(): return (hidden, jnp.stack(k_layers), jnp.stack(v_layers))]
    select_n x1 -> x0, other arithmetic: 22.7 us -> none  [write_token(): jnp.where(positions == cache_len[:, None, None], new_rows[:, None, :], ca...]
    sub x2 -> x0, matrix products: 14.9 us -> none  [attend_rows(): weights = jax.nn.softmax(scores, axis=-1).astype(jnp.bfloat16)]
    all_to_all x3 -> x0, starting transfers between devices: 11.1 us -> none  [the longest x2 7.82 us: device_step(): query = lax.all_to_all(query, 'model', 0, 1, tiled=True)]
    all_to_all x1 -> x0, blocking collectives: 7.41 us -> none  [device_step(): context = lax.all_to_all(context, 'model', 1, 0, tiled=True)]
  transfers between devices with their start and end apart: 5 -> 0, of which waited for: 4 -> 0; matrix products, arithmetic and copies ran while one was open for 29% -> 0% of each run, Pallas kernels for 0% -> 0%
where the time goes in v1:
time: 70.6 us; the launch traced here: 70.5 us
  Pallas kernels  69 us (98%)
  local copies, waits for them, and re-layouts  0.8 us (1%)
    pallas_call x1, Pallas kernels, device_step(): pl.pallas_call(functools.partial(exchange_kernel, layer=layer, last=False...  21 us
    pallas_call x2, Pallas kernels, device_step(): pl.pallas_call(functools.partial(attend_kernel, layer=layer), out_shape=(...  20.3 us
    pallas_call x1, Pallas kernels, device_step(): pl.pallas_call(functools.partial(exchange_kernel, layer=layer, last=True)...  18.1 us
    pallas_call x1, Pallas kernels, device_step(): pl.pallas_call(first_kernel, out_shape=(pltpu.VMEM(hd, BF16), pltpu.VMEM(...  9.62 us

profile of v1, /device:TPU:0, one launch (start us, length us, event | category | flops | bytes accessed | tf_op | source)
XLA Modules:
  0.0 70.5 jit_solution(1034036376672356787)
XLA Ops:
  0.6 0.0 copy-start
  0.6 9.6 %first.1 = (bf16[8,32,256]{2,1,0:T(8,128)(2,1)S(1)}, f32[32,256]{1,0:T(8,128)S(1)}, f32[32,256]{1,0:T(8,128)S(1)}, bf16[32,512,256]{2,1,0:T(8,128)(2,1)S(1)}, bf16[32,512,256]{2,1,0:T(8,128)(2,1)S(1)}) custom-call(bf16[128,2048]{1,0:T(8,128)(2,1)} %refs_1_.1, bf16[2,2048,512]{2,1,0:T(8,128)(2,1)} %refs_3_.1, bf16[2,2048,256]{2,1,0:T(8,128)(2,1)} %refs_4_.1, ...), custom_call_target="tpu_custom_call" | custom-call | tf_op jit(solution)/shard_map/first/pallas_call | solution.py:284
  10.3 0.0 copy-done
  10.3 10.1 %attend0.1 = (bf16[8,32,256]{2,1,0:T(8,128)(2,1)S(1)}, bf16[32,512,256]{2,1,0:T(8,128)(2,1)S(1)}, bf16[32,512,256]{2,1,0:T(8,128)(2,1)S(1)}, bf16[2,32,512,256]{3,2,1,0:T(8,128)(2,1)}, bf16[2,32,512,256]{3,2,1,0:T(8,128)(2,1)}) custom-call(s32[128]{0:T(128)S(1)} %copy-done, ...), custom_call_target="tpu_custom_call", output_to_operand_aliasing={{1}: (4, {}), {2}: (5, {})} | custom-call | tf_op jit(solution)/shard_map/attend0/pallas_call | solution.py:305
  20.4 21.0 %middle.1 = (bf16[8,32,256]{2,1,0:T(8,128)(2,1)S(1)}, f32[32,256]{1,0:T(8,128)S(1)}, f32[32,256]{1,0:T(8,128)S(1)}, bf16[8,32,256]{2,1,0:T(8,128)(2,1)S(1)}, bf1...) custom-call(bf16[8,32,256]{2,1,0:T(8,128)(2,1)S(1)} %get-tuple-element.25.refs_0_, ...), custom_call_target="tpu_custom_call" | custom-call | tf_op jit(solution)/shard_map/middle/pallas_call | solution.py:337
  41.4 10.2 %attend1.1 = (bf16[8,32,256]{2,1,0:T(8,128)(2,1)S(1)}, bf16[32,512,256]{2,1,0:T(8,128)(2,1)S(1)}, bf16[32,512,256]{2,1,0:T(8,128)(2,1)S(1)}, bf16[2,32,512,256]{3,2,1,0:T(8,128)(2,1)}, bf16[2,32,512,256]{3,2,1,0:T(8,128)(2,1)}) custom-call(s32[128]{0:T(128)S(1)} %copy-done, ...), custom_call_target="tpu_custom_call", output_to_operand_aliasing={{1}: (4, {}), {2}: (5, {}), {3}: (6, {}), {4}: (7, {})} | custom-call | tf_op jit(solution)/shard_map/attend1/pallas_call | solution.py:305
  51.6 18.1 %last.1 = bf16[128,2048]{1,0:T(8,128)(2,1)S(1)} custom-call(bf16[8,32,256]{2,1,0:T(8,128)(2,1)S(1)} %get-tuple-element.33.refs_0_, bf16[8,32,256]{2,1,0:T(8,128)(2,1)S(1)} %get-tuple-element.34.refs_1_, bf16[2,512,2048]{2,1,0:T(8,128)(2,1)} %refs_2_.3), custom_call_target="tpu_custom_call" | custom-call | tf_op jit(solution)/shard_map/last/pallas_call | solution.py:326
  69.7 0.8 %copy.24 = bf16[128,2048]{1,0:T(8,128)(2,1)} copy(bf16[128,2048]{1,0:T(8,128)(2,1)S(1)} %last.1) | data formatting | bytes 1048576
Async XLA Ops:
  0.6 9.6 %copy-start = (s32[128]{0:T(128)S(1)}, s32[128]{0:T(128)}, u32[]{:S(2)}) copy-start(s32[128]{0:T(128)} %refs_0_.3) | copy-start | bytes 1540

commit v2 on v1

--- a/solution.py
+++ b/solution.py
@@ -84,9 +84,9 @@
 
 def attend_kernel(*refs, layer):
     if layer:
-        len_ref, q_ref, kn, vn, kb, vb, _, _, ctx, _, _, ko, vo, qs, st, acc, osem = refs
+        len_ref, q_ref, kn, vn, kb, vb, _, _, ctx, _, _, ko, vo, qs, st, osem = refs
     else:
-        len_ref, q_ref, kn, vn, kb, vb, ctx, _, _, ko, vo, qs, st, acc, osem = refs
+        len_ref, q_ref, kn, vn, kb, vb, ctx, _, _, ko, vo, qs, st, osem = refs
     heads, rows, dim = q_ref.shape
     seq = kb.shape[1]
     base = lax.axis_index("model") * rows
@@ -103,42 +103,30 @@
 
     lax.fori_loop(0, rows, patch, 0, unroll=4)
     outs = []
-    step = 4
+    step = 16
     for i in range(rows // step):
         for n, (src, dst) in enumerate(((kb, ko), (vb, vo))):
             c = pltpu.make_async_copy(src.at[pl.ds(i * step, step)], dst.at[layer, pl.ds(i * step, step)], osem.at[n, i])
             c.start()
             outs.append(c)
-    lanes = heads * half
-    lane_b = lax.rem(lax.broadcasted_iota(jnp.int32, (1, lanes), 1), half)
-    row_b = lax.rem(lax.broadcasted_iota(jnp.int32, (lanes, 1), 0), half)
-    pos = lax.broadcasted_iota(jnp.int32, (seq, lanes), 0)
-    for g in range(rows // half):
-        for h in range(heads):
-            qs[h * half:(h + 1) * half, :] = q_ref[h, g * half:(g + 1) * half, :]
-        lens = jnp.zeros((1, lanes), jnp.int32)
-        for b in range(half):
-            lens = jnp.where(lane_b == b, len_ref[base + g * half + b], lens)
-
-        def scores(b, carry):
-            s = lax.dot_general(kb[g * half + b], qs[...], (((1,), (1,)), ((), ())), preferred_element_type=F32)
-            st[...] = jnp.where(lane_b == b, s, st[...])
-            return carry
-
-        lax.fori_loop(0, half, scores, 0, unroll=2)
-        s = jnp.where(pos <= lens, st[...] * (dim ** -0.5), -jnp.inf)
-        e = jnp.exp(s - jnp.max(s, axis=0, keepdims=True))
-        p = e * (1.0 / jnp.sum(e, axis=0, keepdims=True))
-        p = p.T.astype(BF16)
-
-        def mix(b, carry):
-            c = dot(p, vb[g * half + b])
-            acc[...] = jnp.where(row_b == b, c, acc[...])
-            return carry
-
-        lax.fori_loop(0, half, mix, 0, unroll=2)
-        for h in range(heads):
-            ctx[h, g * half:(g + 1) * half, :] = acc[h * half:(h + 1) * half, :].astype(BF16)
+    for h in range(heads):
+        for i in range(dim // 128):
+            qs[i, pl.ds(h, rows, stride=heads), :] = q_ref[h, :, i * 128:(i + 1) * 128].astype(F32)
+    pos = lax.broadcasted_iota(jnp.int32, (heads, seq), 1)
+    for b in range(rows):
+        q = jnp.concatenate([qs[i, b * heads:(b + 1) * heads, :] for i in range(dim // 128)], axis=1).astype(BF16)
+        s = lax.dot_general(q, kb[b], (((1,), (1,)), ((), ())), preferred_element_type=F32)
+        st[b * heads:(b + 1) * heads, :] = jnp.where(pos <= len_ref[base + b], s * (dim ** -0.5), -jnp.inf)
+    for b in range(rows):
+        s = st[b * heads:(b + 1) * heads, :]
+        e = jnp.exp(s - jnp.max(s, axis=1, keepdims=True))
+        p = (e * (1.0 / jnp.sum(e, axis=1, keepdims=True))).astype(BF16)
+        c = dot(p, vb[b])
+        for i in range(dim // 128):
+            qs[i, b * heads:(b + 1) * heads, :] = c[:, i * 128:(i + 1) * 128]
+    for h in range(heads):
+        for i in range(dim // 128):
+            ctx[h, :, i * 128:(i + 1) * 128] = qs[i, pl.ds(h, rows, stride=heads), :].astype(BF16)
     for c in outs:
         c.wait()
 
@@ -310,8 +298,7 @@
                 out_specs=(VM, VM, VM, HBM, HBM),
                 input_output_aliases={4: 1, 5: 2, 6: 3, 7: 4} if layer else {4: 1, 5: 2},
                 scratch_shapes=[
-                    pltpu.VMEM((heads * 16, dim), BF16), pltpu.VMEM((seq, heads * 16), F32),
-                    pltpu.VMEM((heads * 16, dim), F32), DMA((2, rows // 4)),
+                    pltpu.VMEM((dim // 128, rows * heads, 128), F32), pltpu.VMEM((rows * heads, seq), F32), DMA((2, rows // 16)),
                 ],
                 compiler_params=pltpu.CompilerParams(vmem_limit_bytes=8 << 20),
                 name=f"attend{layer}",

time: 70.6 us -> 67.2 us (0.952)
  Pallas kernels: 69 us -> 65.6 us
    pallas_call x2, Pallas kernels: 20.3 us -> 16.9 us  [device_step(): pl.pallas_call(functools.partial(attend_kernel, layer=layer), out_shape=(...]
where the time goes in v2:
time: 67.2 us; the launch traced here: 67.1 us
  Pallas kernels  65.6 us (98%)
  local copies, waits for them, and re-layouts  0.8 us (1%)
  between operations  0.69 us (1%)
    pallas_call x1, Pallas kernels, device_step(): pl.pallas_call(functools.partial(exchange_kernel, layer=layer, last=False...  21 us
    pallas_call x1, Pallas kernels, device_step(): pl.pallas_call(functools.partial(exchange_kernel, layer=layer, last=True)...  18.1 us
    pallas_call x2, Pallas kernels, device_step(): pl.pallas_call(functools.partial(attend_kernel, layer=layer), out_shape=(...  16.9 us
    pallas_call x1, Pallas kernels, device_step(): pl.pallas_call(first_kernel, out_shape=(pltpu.VMEM(hd, BF16), pltpu.VMEM(...  9.62 us

profile of v2, /device:TPU:0, one launch (start us, length us, event | category | flops | bytes accessed | tf_op | source)
XLA Modules:
  0.0 67.1 jit_solution(11424132903299632741)
XLA Ops:
  0.6 0.0 copy-start
  0.6 9.6 %first.1 = (bf16[8,32,256]{2,1,0:T(8,128)(2,1)S(1)}, f32[32,256]{1,0:T(8,128)S(1)}, f32[32,256]{1,0:T(8,128)S(1)}, bf16[32,512,256]{2,1,0:T(8,128)(2,1)S(1)}, bf16[32,512,256]{2,1,0:T(8,128)(2,1)S(1)}) custom-call(bf16[128,2048]{1,0:T(8,128)(2,1)} %refs_1_.1, bf16[2,2048,512]{2,1,0:T(8,128)(2,1)} %refs_3_.1, bf16[2,2048,256]{2,1,0:T(8,128)(2,1)} %refs_4_.1, ...), custom_call_target="tpu_custom_call" | custom-call | tf_op jit(solution)/shard_map/first/pallas_call | solution.py:272
  10.3 0.0 copy-done
  10.3 7.8 %attend0.1 = (bf16[8,32,256]{2,1,0:T(8,128)(2,1)S(1)}, bf16[32,512,256]{2,1,0:T(8,128)(2,1)S(1)}, bf16[32,512,256]{2,1,0:T(8,128)(2,1)S(1)}, bf16[2,32,512,256]{3,2,1,0:T(8,128)(2,1)}, bf16[2,32,512,256]{3,2,1,0:T(8,128)(2,1)}) custom-call(s32[128]{0:T(128)S(1)} %copy-done, ...), custom_call_target="tpu_custom_call", output_to_operand_aliasing={{1}: (4, {}), {2}: (5, {})} | custom-call | tf_op jit(solution)/shard_map/attend0/pallas_call | solution.py:293
  18.1 21.0 %middle.1 = (bf16[8,32,256]{2,1,0:T(8,128)(2,1)S(1)}, f32[32,256]{1,0:T(8,128)S(1)}, f32[32,256]{1,0:T(8,128)S(1)}, bf16[8,32,256]{2,1,0:T(8,128)(2,1)S(1)}, bf1...) custom-call(bf16[8,32,256]{2,1,0:T(8,128)(2,1)S(1)} %get-tuple-element.25.refs_0_, ...), custom_call_target="tpu_custom_call" | custom-call | tf_op jit(solution)/shard_map/middle/pallas_call | solution.py:324
  39.1 9.1 %attend1.1 = (bf16[8,32,256]{2,1,0:T(8,128)(2,1)S(1)}, bf16[32,512,256]{2,1,0:T(8,128)(2,1)S(1)}, bf16[32,512,256]{2,1,0:T(8,128)(2,1)S(1)}, bf16[2,32,512,256]{3,2,1,0:T(8,128)(2,1)}, bf16[2,32,512,256]{3,2,1,0:T(8,128)(2,1)}) custom-call(s32[128]{0:T(128)S(1)} %copy-done, ...), custom_call_target="tpu_custom_call", output_to_operand_aliasing={{1}: (4, {}), {2}: (5, {}), {3}: (6, {}), {4}: (7, {})} | custom-call | tf_op jit(solution)/shard_map/attend1/pallas_call | solution.py:293
  48.2 18.1 %last.1 = bf16[128,2048]{1,0:T(8,128)(2,1)S(1)} custom-call(bf16[8,32,256]{2,1,0:T(8,128)(2,1)S(1)} %get-tuple-element.33.refs_0_, bf16[8,32,256]{2,1,0:T(8,128)(2,1)S(1)} %get-tuple-element.34.refs_1_, bf16[2,512,2048]{2,1,0:T(8,128)(2,1)} %refs_2_.3), custom_call_target="tpu_custom_call" | custom-call | tf_op jit(solution)/shard_map/last/pallas_call | solution.py:313
  66.3 0.8 %copy.24 = bf16[128,2048]{1,0:T(8,128)(2,1)} copy(bf16[128,2048]{1,0:T(8,128)(2,1)S(1)} %last.1) | data formatting | bytes 1048576
Async XLA Ops:
  0.6 9.6 %copy-start = (s32[128]{0:T(128)S(1)}, s32[128]{0:T(128)}, u32[]{:S(2)}) copy-start(s32[128]{0:T(128)} %refs_0_.3) | copy-start | bytes 1540

commit v3 on v0

v3 whole, which is shorter than its diff:
```python
import functools

import jax
import jax.numpy as jnp
from jax import lax
from jax.experimental import pallas as pl
from jax.experimental.pallas import tpu as pltpu
from jax.sharding import PartitionSpec as P

F32 = jnp.float32
BF16 = jnp.bfloat16
MESH = pl.DeviceIdType.MESH
HBM = pl.BlockSpec(memory_space=pltpu.HBM)
VM = pl.BlockSpec(memory_space=pltpu.VMEM)
SM = pl.BlockSpec(memory_space=pltpu.SMEM)
DMA = pltpu.SemaphoreType.DMA


def dot(a, b):
    return jnp.dot(a, b, preferred_element_type=F32)


def place():
    m = lax.axis_index("model")
    return lax.axis_index("replica"), m, lax.rem(m, 2), m // 2


def meet(peers):
    barrier = pltpu.get_barrier_semaphore()
    for peer in peers:
        pl.semaphore_signal(barrier, inc=1, device_id=peer, device_id_type=MESH)
    pl.semaphore_wait(barrier, len(peers))


def send(src, dst, send_sem, recv_sem, peer):
    return pltpu.make_async_remote_copy(
        src_ref=src, dst_ref=dst, send_sem=send_sem, recv_sem=recv_sem, device_id=peer, device_id_type=MESH)


def scatter_queries(get, qs, heads, rows):
    for h in range(heads):
        for i in range(2):
            qs[i, pl.ds(h, rows, stride=heads), :] = get(h)[:, i * 128:(i + 1) * 128].astype(F32)


def attend_rows(which, heads, length, kb, vb, qs, st, new=None):
    seq, dim = kb.shape[1:]
    scale = dim ** -0.5
    pos = lax.broadcasted_iota(jnp.int32, (heads, seq), 1)
    for b in which:
        cut = slice(b * heads, (b + 1) * heads)
        q = jnp.concatenate([qs[i, cut, :] for i in range(2)], axis=1)
        s = lax.dot_general(q.astype(BF16), kb[b], (((1,), (1,)), ((), ())), preferred_element_type=F32)
        if new is not None:
            s = jnp.where(pos == length(b), jnp.sum(q * new[0][b:b + 1, :], axis=1, keepdims=True), s)
        s = jnp.where(pos <= length(b), s * scale, -jnp.inf)
        for i in range(2):
            st[4 * i + b // 8, b % 8 * heads:(b % 8 + 1) * heads, :] = s[:, i * 256:(i + 1) * 256]
    for b in which:
        cut = slice(b * heads, (b + 1) * heads)
        s = jnp.concatenate([st[4 * i + b // 8, b % 8 * heads:(b % 8 + 1) * heads, :] for i in range(2)], axis=1)
        e = jnp.exp(s - jnp.max(s, axis=1, keepdims=True))
        p = (e * (1.0 / jnp.sum(e, axis=1, keepdims=True))).astype(BF16)
        if new is None:
            c = dot(p, vb[b])
        else:
            here = pos == length(b)
            p = p.astype(F32)
            mine = jnp.sum(jnp.where(here, p, 0.0), axis=1, keepdims=True)
            c = dot(jnp.where(here, 0.0, p).astype(BF16), vb[b]) + mine * new[1][b:b + 1, :]
        for i in range(2):
            qs[i, cut, :] = c[:, i * 128:(i + 1) * 128]


def gather_contexts(ctx, qs, first, count, heads):
    for h in range(heads):
        for i in range(2):
            ctx[h, first:first + count, i * 128:(i + 1) * 128] = (
                qs[i, pl.ds(first * heads + h, count, stride=heads), :].astype(BF16))


def layer0_kernel(len_ref, x_hbm, wq_hbm, wk_hbm, wv_hbm, wo_hbm, kc_hbm, vc_hbm,
                  q_out, kvn, hl, wof, k0, v0, k1, v1,
                  xs, qown, qrecv, qs, ctx, wos, lhs, ys, yrecv, wq1, qacc, q1own, q1recv, stage,
                  wsem, lsem, csem, qsem, gsem, psem, ysem, hsem, q1sem, xsem, yzsem, msem):
    rep, m, core, chip = place()
    heads, rows, dim = q_out.shape
    half = rows // 2
    chunks = hl.shape[0]
    across_m, mate_m, diag_m = lax.rem(m + 2, 4), m + 1 - 2 * core, 3 - m
    across, mate, diag = (rep, across_m), (rep, mate_m), (rep, diag_m)
    rep_y, rep_z, rep_yz = rep + 1 - 2 * lax.rem(rep, 2), lax.rem(rep + 2, 4), 3 - rep
    next_y, next_z = (rep_y, m), (rep_z, m)
    span = wof.shape[2]
    quarter = stage.shape[0]
    sub = quarter // 2

    def piece(owner, r, s):
        start = pl.multiple_of(lax.rem(r, 2) * quarter + s * sub, sub)
        return wof.at[2 * owner + r // 2, pl.ds(start, sub), :]

    load_x = pltpu.make_async_copy(x_hbm, xs, wsem.at[0])
    load_x.start()
    deep = k1.shape[1]
    blocks = xs.shape[1] // deep
    loads = []
    for n, src in enumerate((wq_hbm.at[0, :, pl.ds(0, dim)], wq_hbm.at[0, :, pl.ds(dim, dim)], wk_hbm.at[0], wv_hbm.at[0])):
        loads.append([pltpu.make_async_copy(src.at[pl.ds(t * deep, deep)], k1.at[n * blocks + t], lsem.at[n, t])
                      for t in range(blocks)])
        for c in loads[n]:
            c.start()

    def first_weights(n, rows_ref):
        total = None
        for t in range(blocks):
            loads[n][t].wait()
            part = dot(rows_ref[:, t * deep:(t + 1) * deep], k1[n * blocks + t])
            total = part if t == 0 else total + part
        return total.astype(BF16)

    theirs = pl.ds(pl.multiple_of((1 - chip) * span, span), span)
    ours = pl.ds(pl.multiple_of(chip * span, span), span)
    load_stage = pltpu.make_async_copy(
        wo_hbm.at[1, pl.ds(pl.multiple_of(rep * quarter, quarter), quarter), theirs], stage, wsem.at[5])
    load_stage.start()
    meet((across, diag, mate, next_y, next_z))
    load_x.wait()
    qcopies = []
    for i in range(2):
        q = first_weights(i, xs)
        for d in range(4):
            qown[d, i] = q[d * rows:(d + 1) * rows]
        for n, (peer, who) in enumerate(((across, across_m), (diag, diag_m), (mate, mate_m))):
            c = send(qown.at[who, i], qrecv.at[m, i], qsem.at[0, n, i], qsem.at[1, n, i], peer)
            c.start()
            qcopies.append(c)
        qrecv[m, i] = qown[m, i]
    loads0 = [pltpu.make_async_copy(kc_hbm.at[0], k0, csem.at[0]), pltpu.make_async_copy(vc_hbm.at[0], v0, csem.at[1])]
    load_wo = pltpu.make_async_copy(wo_hbm.at[0], wos.at[core], wsem.at[6])
    load_q1 = pltpu.make_async_copy(wq_hbm.at[1], wq1.at[core], wsem.at[7])
    load_own = [pltpu.make_async_copy(wo_hbm.at[1, pl.ds(i * dim, dim), ours], wof.at[2 * m + i], wsem.at[8 + i])
                for i in range(2)]
    for c in loads0 + [load_wo, load_q1] + load_own:
        c.start()
    load_stage.wait()
    xcopies = []
    for s in range(2):
        c = send(stage.at[pl.ds(s * sub, sub)], piece(m, rep, s), xsem.at[0, s], xsem.at[1, s], across)
        c.start()
        xcopies.append(c)
    mine = xs[pl.ds(pl.multiple_of(m * rows, rows), rows), :]
    kvn[0] = first_weights(2, mine).astype(F32)
    kvn[1] = first_weights(3, mine).astype(F32)
    for c in qcopies:
        c.wait()
    scatter_queries(lambda h: qrecv[h // 2, h % 2], qs, heads, rows)
    loads0[0].wait()
    loads0[1].wait()
    loads1 = [pltpu.make_async_copy(kc_hbm.at[1], k1, csem.at[2]), pltpu.make_async_copy(vc_hbm.at[1], v1, csem.at[3])]
    for c in loads1:
        c.start()
    base = m * rows
    load_wo.wait()
    push_wo = send(wos.at[core], wos.at[core], psem.at[0, 0], psem.at[1, 0], mate)
    push_wo.start()
    load_q1.wait()
    push_q1 = send(wq1.at[core], wq1.at[core], psem.at[0, 1], psem.at[1, 1], mate)
    push_q1.start()
    gives = []
    for g in range(2):
        attend_rows(range(g * half, (g + 1) * half), heads, lambda b: len_ref[base + b], k0, v0, qs, ys, (kvn.at[0], kvn.at[1]))
        gather_contexts(ctx, qs, g * half, half, heads)
        c = send(ctx.at[pl.ds((1 - chip) * 4, 4), pl.ds(g * half, half), :],
                 lhs.at[:, pl.ds(rows + g * half, half), :], gsem.at[0, g], gsem.at[1, g], across)
        c.start()
        gives.append(c)
    for i in range(4):
        lhs[i, 0:rows, :] = ctx[chip * 4 + i]
    mcopies = []

    def to_mate(ref):
        n = len(mcopies)
        c = send(ref, ref, msem.at[0, n], msem.at[1, n], mate)
        c.start()
        mcopies.append(c)

    around = []
    for s in range(2):
        xcopies[s].wait_recv()
        for n, peer in enumerate((next_y, next_z)):
            ref = piece(across_m, rep, s)
            c = send(ref, ref, yzsem.at[0, n, s], yzsem.at[1, n, s], peer)
            c.start()
            around.append(c)
    push_wo.wait()
    for c in gives:
        c.wait()
    ycopies = []
    for j in range(chunks):
        y = dot(lhs[0], wos[0, 0:256, j * 256:(j + 1) * 256])
        for i in range(1, 4):
            y += dot(lhs[i], wos[i // 2, (i % 2) * 256:(i % 2 + 1) * 256, j * 256:(j + 1) * 256])
        ys[j] = y
        c = send(ys.at[j, pl.ds(rows, rows)], yrecv.at[j], ysem.at[0, j], ysem.at[1, j], across)
        c.start()
        ycopies.append(c)
    loads_kv = [[pltpu.make_async_copy(src.at[1, pl.ds(j * dim, dim)], wos.at[0, pl.ds(n * dim, dim), pl.ds(j * dim, dim)],
                                       lsem.at[4 + n, j]) for j in range(chunks)] for n, src in enumerate((wk_hbm, wv_hbm))]
    for c in loads_kv[0] + loads_kv[1]:
        c.start()
    for i in range(2):
        load_own[i].wait()
        to_mate(wof.at[2 * m + i])
    for s in range(2):
        to_mate(piece(across_m, rep, s))
    hcopies = []
    for j in range(chunks):
        ycopies[j].wait_recv()
        old = xs[pl.ds(pl.multiple_of(m * rows, rows), rows), j * 256:(j + 1) * 256]
        hl[j, 0:rows, :] = (old.astype(F32) + (ys[j, 0:rows, :] + yrecv[j])).astype(BF16)
        c = send(hl.at[j, pl.ds(0, rows)], hl.at[j, pl.ds(rows, rows)], hsem.at[0, j], hsem.at[1, j], across)
        c.start()
        hcopies.append(c)
    for c in around:
        c.wait_recv()
    for s, (n, peer, other) in enumerate(((1, next_z, rep_y), (0, next_y, rep_z))):
        ref = piece(across_m, other, s)
        c = send(ref, ref, yzsem.at[0, n, 2], yzsem.at[1, n, 2], peer)
        c.start()
        around.append(c)
    for other in (rep_y, rep_z):
        for s in range(2):
            to_mate(piece(across_m, other, s))
    push_q1.wait()
    for j in range(chunks):
        hcopies[j].wait_recv()
        for i in range(4):
            part = dot(hl[j], wq1[i // 2, j * 256:(j + 1) * 256, (i % 2) * 256:(i % 2 + 1) * 256])
            if j == 0:
                qacc[i] = part
            else:
                qacc[i] += part
    q1copies = []
    for i in range(4):
        q1own[i] = qacc[i].astype(BF16)
        c = send(q1own.at[i, pl.ds(rows, rows)], q1recv.at[i], q1sem.at[0, i], q1sem.at[1, i], across)
        c.start()
        q1copies.append(c)
    for n in range(2):
        for j in range(chunks):
            loads_kv[n][j].wait()
            part = dot(hl[j, 0:rows, :], wos[0, n * dim:(n + 1) * dim, j * dim:(j + 1) * dim])
            t = part if j == 0 else t + part
        kvn[2 + n] = t.astype(BF16).astype(F32)
    for i in range(4):
        q_out[chip * 4 + i] = q1own[i, 0:rows, :]
    for s in range(2):
        around[4 + s].wait_recv()
    for s in range(2):
        to_mate(piece(across_m, rep_yz, s))
    for i in range(4):
        q1copies[i].wait_recv()
        q_out[(1 - chip) * 4 + i] = q1recv[i]
    for c in mcopies:
        c.wait()
    for c in xcopies + around + ycopies + hcopies + q1copies:
        c.wait_send()
    for c in loads1:
        c.wait()


def attend1_kernel(len_ref, q_ref, kvn, k0, v0, k1, v1, ctx, _k0, _v0, _k1, _v1, ko, vo, qs, st, osem):
    heads, rows, dim = q_ref.shape
    base = lax.axis_index("model") * rows
    tile = 16
    outs = []
    for layer, bufs in enumerate(((k0, v0), (k1, v1))):
        def patch(b, carry):
            ln = len_ref[base + b]
            start = pl.multiple_of((ln // tile) * tile, tile)
            hit = lax.broadcasted_iota(jnp.int32, (tile, dim), 0) == ln - start
            for n, buf in enumerate(bufs):
                old = buf[b, pl.ds(start, tile), :].astype(F32)
                buf[b, pl.ds(start, tile), :] = jnp.where(hit, kvn[2 * layer + n, pl.ds(b, 1), :], old).astype(BF16)
            return carry

        lax.fori_loop(0, rows, patch, 0, unroll=4)
        for i in range(2):
            for n, (src, dst) in enumerate(zip(bufs, (ko, vo))):
                part = pl.ds(i * (rows // 2), rows // 2)
                c = pltpu.make_async_copy(src.at[part], dst.at[layer, part], osem.at[layer, n, i])
                c.start()
                outs.append(c)
    scatter_queries(lambda h: q_ref[h], qs, heads, rows)
    attend_rows(range(rows), heads, lambda b: len_ref[base + b], k1, v1, qs, st)
    gather_contexts(ctx, qs, 0, rows, heads)
    for c in outs:
        c.wait()


def last_kernel(ctx, hid, wof, out, other, acc, hl, pl2, gsem, hsem, psem):
    rep, m, core, chip = place()
    across_m, mate_m = lax.rem(m + 2, 4), m + 1 - 2 * core
    across, mate = (rep, across_m), (rep, mate_m)
    heads, rows, dim = ctx.shape
    chunks = hl.shape[0]
    cols = chunks // 2
    meet((across, mate))
    gives = []
    for p in range(4):
        two = pl.ds(2 * p, 2)
        c = send(ctx.at[two], other.at[two], gsem.at[0, p], gsem.at[1, p], across)
        c.start()
        gives.append(c)
    hcopies = []
    pcopies = []

    def to_mate(at):
        n = len(pcopies)
        c = send(hl.at[at], pl2.at[at], psem.at[0, n], psem.at[1, n], mate)
        c.start()
        pcopies.append(c)

    for p in range(4):
        gives[p].wait_recv()
        left = [jnp.concatenate((ctx[2 * p + i], other[2 * p + i]), axis=0) for i in range(2)]
        for j in range(cols):
            part = dot(left[0], wof[2 * p, :, j * dim:(j + 1) * dim]) + dot(left[1], wof[2 * p + 1, :, j * dim:(j + 1) * dim])
            if p == 0:
                acc[j] = part
            elif p < 3:
                acc[j] += part
            else:
                at = chip * cols + j
                hl[at] = (hid[at].astype(F32) + (acc[j] + part)).astype(BF16)
                for n in range(2):
                    c = send(hl.at[at, pl.ds(n * rows, rows)], hl.at[at, pl.ds((1 - n) * rows, rows)],
                             hsem.at[0, n, j], hsem.at[1, n, j], across)
                    c.start()
                    hcopies.append(c)
                to_mate(at)
    for j in range(cols):
        for n in range(2):
            hcopies[2 * j + n].wait_recv()
        to_mate((1 - chip) * cols + j)

    def put(who, at, value):
        out[pl.ds(pl.multiple_of(who * rows, rows), rows), at * dim:(at + 1) * dim] = value

    for j in range(chunks):
        put(m, j, hl[j, 0:rows, :])
        put(across_m, j, hl[j, rows:2 * rows, :])
    for c in pcopies:
        c.wait_recv()
    for j in range(chunks):
        put(mate_m, j, pl2[j, 0:rows, :])
        put(3 - m, j, pl2[j, rows:2 * rows, :])
    for c in gives + hcopies + pcopies:
        c.wait_send()


def solution(mesh):
    row_axes = ("replica", "model")
    cache_spec = P(None, row_axes, None, None)

    def device_step(x, cache_len, w_query, w_key, w_value, w_out, k_cache, v_cache):
        layers, rows, seq, dim = k_cache.shape
        total, width = x.shape
        chunks = width // dim
        local = w_query.shape[-1]
        heads = local // dim * mesh.shape["model"]
        hd = (heads, rows, dim)
        x, w_query, w_key, w_value, w_out, k_cache, v_cache = (
            pltpu.with_memory_space_constraint(a, pltpu.HBM)
            for a in (x, w_query, w_key, w_value, w_out, k_cache, v_cache))
        remote = functools.partial(pltpu.CompilerParams, has_side_effects=True)
        cache = pltpu.VMEM((rows, seq, dim), BF16)
        qs = pltpu.VMEM((2, rows * heads, 128), F32)
        st = pltpu.VMEM((chunks, 2 * rows, dim), F32)

        q, kvn, hid, wof, *caches = pl.pallas_call(
            layer0_kernel,
            out_shape=(pltpu.VMEM(hd, BF16), pltpu.VMEM((4, rows, dim), F32), pltpu.VMEM((chunks, 2 * rows, dim), BF16),
                       pltpu.VMEM((heads, dim, width // 2), BF16)) + (cache,) * 4,
            in_specs=[SM] + [HBM] * 7,
            out_specs=(VM,) * 8,
            scratch_shapes=[
                pltpu.VMEM((total, width), BF16),
                pltpu.VMEM((4, 2, rows, dim), BF16), pltpu.VMEM((4, 2, rows, dim), BF16),
                qs, pltpu.VMEM(hd, BF16),
                pltpu.VMEM((2, local, width), BF16), pltpu.VMEM((4, 2 * rows, dim), BF16),
                pltpu.VMEM((chunks, 2 * rows, dim), F32), pltpu.VMEM((chunks, rows, dim), F32),
                pltpu.VMEM((2, width, local), BF16),
                pltpu.VMEM((4, 2 * rows, dim), F32), pltpu.VMEM((4, 2 * rows, dim), BF16),
                pltpu.VMEM((4, rows, dim), BF16), pltpu.VMEM((local // 4, width // 2), BF16),
                DMA((10,)), DMA((6, 8)), DMA((4,)), DMA((2, 3, 2)), DMA((2, 2)), DMA((2, 2)), DMA((2, chunks)), DMA((2, chunks)),
                DMA((2, 4)), DMA((2, 2)), DMA((2, 2, 3)), DMA((2, 10)),
            ],
            compiler_params=remote(collective_id=0, vmem_limit_bytes=11 << 20),
            name="layer0",
        )(cache_len, x, w_query, w_key, w_value, w_out, k_cache, v_cache)

        ctx, _, _, _, _, ko, vo = pl.pallas_call(
            attend1_kernel,
            out_shape=(pltpu.VMEM(hd, BF16), cache, cache, cache, cache,
                       jax.ShapeDtypeStruct(k_cache.shape, BF16), jax.ShapeDtypeStruct(v_cache.shape, BF16)),
            in_specs=[SM] + [VM] * 6,
            out_specs=(VM,) * 5 + (HBM, HBM),
            input_output_aliases={3: 1, 4: 2, 5: 3, 6: 4},
            scratch_shapes=[qs, st, DMA((2, 2, 2))],
            compiler_params=pltpu.CompilerParams(vmem_limit_bytes=3 << 20),
            name="attend1",
        )(cache_len, q, kvn, *caches)

        out = pl.pallas_call(
            last_kernel,
            out_shape=pltpu.VMEM((total, width), BF16),
            in_specs=[VM] * 3,
            out_specs=VM,
            scratch_shapes=[
                pltpu.VMEM(hd, BF16), pltpu.VMEM((chunks // 2, 2 * rows, dim), F32),
                pltpu.VMEM((chunks, 2 * rows, dim), BF16), pltpu.VMEM((chunks, 2 * rows, dim), BF16),
                DMA((2, 4)), DMA((2, 2, chunks // 2)), DMA((2, chunks)),
            ],
            compiler_params=remote(collective_id=1, vmem_limit_bytes=4 << 20),
            name="last",
        )(ctx, hid, wof)
        return out, ko, vo

    return jax.shard_map(
        device_step,
        mesh=mesh,
        in_specs=(P("replica", None), P("replica"), P(None, None, "model"), P(), P(), P(None, "model", None), cache_spec, cache_spec),
        out_specs=(P("replica", None), cache_spec, cache_spec),
        check_vma=False,
    )
```

time: 175 us -> 60.5 us (0.35)
  Pallas kernels: 0 us -> 58.3 us
  other arithmetic: 49 us -> 0 us
  waiting for transfers between devices: 48.1 us -> 0 us
  matrix products: 40.7 us -> 0 us
  between operations: 14.2 us -> 0.67 us
  starting transfers between devices: 11.2 us -> 0 us
  blocking collectives: 7.41 us -> 0 us
  local copies, waits for them, and re-layouts: 3.45 us -> 1.44 us
    pallas_call x0 -> x3, Pallas kernels: none -> 58.3 us  [the longest x1 34.7 us: device_step(): pl.pallas_call(layer0_kernel, out_shape=(pltpu.VMEM(hd, BF16), pltpu.VMEM...]
    psum x2 -> x0, waiting for transfers between devices: 44.8 us -> none  [device_step(): total = lax.psum(part_sum, 'model')]
    dot_general x10 -> x0, matrix products: 25.8 us -> none  [the longest x2 12.1 us: attend_rows(): jnp.einsum('bhs,bsd->bhd', weights, v_layer, preferred_element_type=jnp.f...]
    another operation x1 -> x0, other arithmetic: 22.8 us -> none  [device_step(): return (hidden, jnp.stack(k_layers), jnp.stack(v_layers))]
    select_n x1 -> x0, other arithmetic: 22.7 us -> none  [write_token(): jnp.where(positions == cache_len[:, None, None], new_rows[:, None, :], ca...]
    sub x2 -> x0, matrix products: 14.9 us -> none  [attend_rows(): weights = jax.nn.softmax(scores, axis=-1).astype(jnp.bfloat16)]
    all_to_all x3 -> x0, starting transfers between devices: 11.1 us -> none  [the longest x2 7.82 us: device_step(): query = lax.all_to_all(query, 'model', 0, 1, tiled=True)]
    all_to_all x1 -> x0, blocking collectives: 7.41 us -> none  [device_step(): context = lax.all_to_all(context, 'model', 1, 0, tiled=True)]
  transfers between devices with their start and end apart: 5 -> 0, of which waited for: 4 -> 0; matrix products, arithmetic and copies ran while one was open for 29% -> 0% of each run, Pallas kernels for 0% -> 0%
where the time goes in v3:
time: 60.5 us; the launch traced here: 60.4 us
  Pallas kernels  58.3 us (96%)
  local copies, waits for them, and re-layouts  1.44 us (2%)
  between operations  0.67 us (1%)
    pallas_call x1, Pallas kernels, device_step(): pl.pallas_call(layer0_kernel, out_shape=(pltpu.VMEM(hd, BF16), pltpu.VMEM...  34.7 us
    pallas_call x1, Pallas kernels, device_step(): pl.pallas_call(attend1_kernel, out_shape=(pltpu.VMEM(hd, BF16), cache, ca...  11.9 us
    pallas_call x1, Pallas kernels, device_step(): pl.pallas_call(last_kernel, out_shape=pltpu.VMEM((total, width), BF16), i...  11.6 us
    unnamed x3, local copies, waits for them, and re-layouts  1.44 us

profile of v3, /device:TPU:0, one launch (start us, length us, event | category | flops | bytes accessed | tf_op | source)
XLA Modules:
  0.0 60.4 jit_solution(17620758772629325308)
XLA Ops:
  0.6 0.0 copy-start
  0.6 0.6 %copy-done = s32[128]{0:T(128)S(1)} copy-done((s32[128]{0:T(128)S(1)}, s32[128]{0:T(128)}, u32[]{:S(2)}) %copy-start) | copy-done | bytes 536
  1.3 34.7 %layer0.1 = (bf16[8,32,256]{2,1,0:T(8,128)(2,1)S(1)}, f32[4,32,256]{2,1,0:T(8,128)S(1)}, bf16[8,64,256]{2,1,0:T(8,128)(2,1)S(1)}, bf16[8,256,1024]{2,1,0:T(8,128...) custom-call(s32[128]{0:T(128)S(1)} %copy-done, ...), custom_call_target="tpu_custom_call" | custom-call | tf_op jit(solution)/shard_map/layer0/pallas_call | solution.py:381
  36.0 11.9 %attend1.1 = (bf16[8,32,256]{2,1,0:T(8,128)(2,1)S(1)}, bf16[32,512,256]{2,1,0:T(8,128)(2,1)S(1)}, bf16[32,512,256]{2,1,0:T(8,128)(2,1)S(1)}, bf16[32,512,256]{2,...) custom-call(s32[128]{0:T(128)S(1)} %copy-done, ...), custom_call_target="tpu_custom_call", output_to_operand_aliasing={{1}: (3, {}), {2}: (4, {}), {3}: (5, {}), {4}: (6, {})} | custom-call | tf_op jit(solution)/shard_map/attend1/pallas_call | solution.py:403
  48.0 11.6 %last.1 = bf16[128,2048]{1,0:T(8,128)(2,1)S(1)} custom-call(bf16[8,32,256]{2,1,0:T(8,128)(2,1)S(1)} %get-tuple-element.20.ctx, bf16[8,64,256]{2,1,0:T(8,128)(2,1)S(1)} %get-tuple-element.21.hid, bf16[8,256,1024]{2,1,0:T(8,128)(2,1)S(1)} %get-tuple-element.22.wof), custom_call_target="tpu_custom_call" | custom-call | tf_op jit(solution)/shard_map/last/pallas_call | solution.py:415
  59.6 0.8 %copy.20 = bf16[128,2048]{1,0:T(8,128)(2,1)} copy(bf16[128,2048]{1,0:T(8,128)(2,1)S(1)} %last.1) | data formatting | bytes 1048576
Async XLA Ops:
  0.6 0.7 %copy-start = (s32[128]{0:T(128)S(1)}, s32[128]{0:T(128)}, u32[]{:S(2)}) copy-start(s32[128]{0:T(128)} %len_ref.3) | copy-start | bytes 1540

commit v4 on v3

--- a/solution.py
+++ b/solution.py
@@ -25,11 +25,14 @@
     return lax.axis_index("replica"), m, lax.rem(m, 2), m // 2
 
 
-def meet(peers):
+def greet(peers):
     barrier = pltpu.get_barrier_semaphore()
     for peer in peers:
         pl.semaphore_signal(barrier, inc=1, device_id=peer, device_id_type=MESH)
-    pl.semaphore_wait(barrier, len(peers))
+
+
+def meet(peers):
+    pl.semaphore_wait(pltpu.get_barrier_semaphore(), len(peers))
 
 
 def send(src, dst, send_sem, recv_sem, peer):
@@ -43,7 +46,7 @@
             qs[i, pl.ds(h, rows, stride=heads), :] = get(h)[:, i * 128:(i + 1) * 128].astype(F32)
 
 
-def attend_rows(which, heads, length, kb, vb, qs, st, new=None):
+def attend_rows(which, heads, length, kb, vb, qs, st, new=None, values=None):
     seq, dim = kb.shape[1:]
     scale = dim ** -0.5
     pos = lax.broadcasted_iota(jnp.int32, (heads, seq), 1)
@@ -56,6 +59,8 @@
         s = jnp.where(pos <= length(b), s * scale, -jnp.inf)
         for i in range(2):
             st[4 * i + b // 8, b % 8 * heads:(b % 8 + 1) * heads, :] = s[:, i * 256:(i + 1) * 256]
+    if values is not None:
+        values.wait()
     for b in which:
         cut = slice(b * heads, (b + 1) * heads)
         s = jnp.concatenate([st[4 * i + b // 8, b % 8 * heads:(b % 8 + 1) * heads, :] for i in range(2)], axis=1)
@@ -93,11 +98,31 @@
     next_y, next_z = (rep_y, m), (rep_z, m)
     span = wof.shape[2]
     quarter = stage.shape[0]
-    sub = quarter // 2
+    subs = 4
+    sub = quarter // subs
 
     def piece(owner, r, s):
         start = pl.multiple_of(lax.rem(r, 2) * quarter + s * sub, sub)
         return wof.at[2 * owner + r // 2, pl.ds(start, sub), :]
+
+    friends = (across, diag, mate, next_y, next_z)
+    greet(friends)
+    xcopies = []
+
+    def send_quarter(s):
+        c = send(stage.at[pl.ds(s * sub, sub)], piece(m, rep, s), xsem.at[0, s], xsem.at[1, s], across)
+        c.start()
+        xcopies.append(c)
+
+    around = []
+
+    def pass_round(s):
+        xcopies[s].wait_recv()
+        ref = piece(across_m, rep, s)
+        for n, peer in enumerate((next_y, next_z)):
+            c = send(ref, ref, yzsem.at[0, n, s], yzsem.at[1, n, s], peer)
+            c.start()
+            around.append(c)
 
     load_x = pltpu.make_async_copy(x_hbm, xs, wsem.at[0])
     load_x.start()
@@ -107,8 +132,12 @@
     for n, src in enumerate((wq_hbm.at[0, :, pl.ds(0, dim)], wq_hbm.at[0, :, pl.ds(dim, dim)], wk_hbm.at[0], wv_hbm.at[0])):
         loads.append([pltpu.make_async_copy(src.at[pl.ds(t * deep, deep)], k1.at[n * blocks + t], lsem.at[n, t])
                       for t in range(blocks)])
-        for c in loads[n]:
+
+    def start(copies):
+        for c in copies:
             c.start()
+
+    start(loads[0] + loads[1])
 
     def first_weights(n, rows_ref):
         total = None
@@ -123,11 +152,16 @@
     load_stage = pltpu.make_async_copy(
         wo_hbm.at[1, pl.ds(pl.multiple_of(rep * quarter, quarter), quarter), theirs], stage, wsem.at[5])
     load_stage.start()
-    meet((across, diag, mate, next_y, next_z))
+    loads0 = [pltpu.make_async_copy(kc_hbm.at[0], k0, csem.at[0]), pltpu.make_async_copy(vc_hbm.at[0], v0, csem.at[1])]
     load_x.wait()
+    start(loads[2] + loads[3])
     qcopies = []
     for i in range(2):
         q = first_weights(i, xs)
+        if i == 0:
+            start(loads0[:1])
+            meet(friends)
+            load_stage.wait()
         for d in range(4):
             qown[d, i] = q[d * rows:(d + 1) * rows]
         for n, (peer, who) in enumerate(((across, across_m), (diag, diag_m), (mate, mate_m))):
@@ -135,19 +169,13 @@
             c.start()
             qcopies.append(c)
         qrecv[m, i] = qown[m, i]
-    loads0 = [pltpu.make_async_copy(kc_hbm.at[0], k0, csem.at[0]), pltpu.make_async_copy(vc_hbm.at[0], v0, csem.at[1])]
     load_wo = pltpu.make_async_copy(wo_hbm.at[0], wos.at[core], wsem.at[6])
     load_q1 = pltpu.make_async_copy(wq_hbm.at[1], wq1.at[core], wsem.at[7])
     load_own = [pltpu.make_async_copy(wo_hbm.at[1, pl.ds(i * dim, dim), ours], wof.at[2 * m + i], wsem.at[8 + i])
                 for i in range(2)]
-    for c in loads0 + [load_wo, load_q1] + load_own:
-        c.start()
-    load_stage.wait()
-    xcopies = []
-    for s in range(2):
-        c = send(stage.at[pl.ds(s * sub, sub)], piece(m, rep, s), xsem.at[0, s], xsem.at[1, s], across)
-        c.start()
-        xcopies.append(c)
+    start(loads0[1:])
+    for s in range(subs):
+        send_quarter(s)
     mine = xs[pl.ds(pl.multiple_of(m * rows, rows), rows), :]
     kvn[0] = first_weights(2, mine).astype(F32)
     kvn[1] = first_weights(3, mine).astype(F32)
@@ -155,25 +183,28 @@
         c.wait()
     scatter_queries(lambda h: qrecv[h // 2, h % 2], qs, heads, rows)
     loads0[0].wait()
-    loads0[1].wait()
+    start([load_wo, load_q1] + load_own)
     loads1 = [pltpu.make_async_copy(kc_hbm.at[1], k1, csem.at[2]), pltpu.make_async_copy(vc_hbm.at[1], v1, csem.at[3])]
-    for c in loads1:
-        c.start()
     base = m * rows
-    load_wo.wait()
-    push_wo = send(wos.at[core], wos.at[core], psem.at[0, 0], psem.at[1, 0], mate)
-    push_wo.start()
-    load_q1.wait()
-    push_q1 = send(wq1.at[core], wq1.at[core], psem.at[0, 1], psem.at[1, 1], mate)
-    push_q1.start()
+    pass_round(0)
     gives = []
     for g in range(2):
-        attend_rows(range(g * half, (g + 1) * half), heads, lambda b: len_ref[base + b], k0, v0, qs, ys, (kvn.at[0], kvn.at[1]))
+        attend_rows(range(g * half, (g + 1) * half), heads, lambda b: len_ref[base + b], k0, v0, qs, ys,
+                    (kvn.at[0], kvn.at[1]), loads0[1] if g == 0 else None)
         gather_contexts(ctx, qs, g * half, half, heads)
         c = send(ctx.at[pl.ds((1 - chip) * 4, 4), pl.ds(g * half, half), :],
                  lhs.at[:, pl.ds(rows + g * half, half), :], gsem.at[0, g], gsem.at[1, g], across)
         c.start()
         gives.append(c)
+        if g == 0:
+            start(loads1)
+            load_wo.wait()
+            push_wo = send(wos.at[core], wos.at[core], psem.at[0, 0], psem.at[1, 0], mate)
+            push_wo.start()
+            load_q1.wait()
+            push_q1 = send(wq1.at[core], wq1.at[core], psem.at[0, 1], psem.at[1, 1], mate)
+            push_q1.start()
+            pass_round(1)
     for i in range(4):
         lhs[i, 0:rows, :] = ctx[chip * 4 + i]
     mcopies = []
@@ -184,14 +215,8 @@
         c.start()
         mcopies.append(c)
 
-    around = []
-    for s in range(2):
-        xcopies[s].wait_recv()
-        for n, peer in enumerate((next_y, next_z)):
-            ref = piece(across_m, rep, s)
-            c = send(ref, ref, yzsem.at[0, n, s], yzsem.at[1, n, s], peer)
-            c.start()
-            around.append(c)
+    for s in range(2, subs):
+        pass_round(s)
     push_wo.wait()
     for c in gives:
         c.wait()
@@ -211,8 +236,19 @@
     for i in range(2):
         load_own[i].wait()
         to_mate(wof.at[2 * m + i])
-    for s in range(2):
+    for s in range(subs):
         to_mate(piece(across_m, rep, s))
+    for c in around:
+        c.wait_recv()
+    for s in range(subs):
+        n, peer, other = ((1, next_z, rep_y), (0, next_y, rep_z))[s % 2]
+        ref = piece(across_m, other, s)
+        c = send(ref, ref, yzsem.at[0, n, subs + s // 2], yzsem.at[1, n, subs + s // 2], peer)
+        c.start()
+        around.append(c)
+    for other in (rep_y, rep_z):
+        for s in range(subs):
+            to_mate(piece(across_m, other, s))
     hcopies = []
     for j in range(chunks):
         ycopies[j].wait_recv()
@@ -221,16 +257,6 @@
         c = send(hl.at[j, pl.ds(0, rows)], hl.at[j, pl.ds(rows, rows)], hsem.at[0, j], hsem.at[1, j], across)
         c.start()
         hcopies.append(c)
-    for c in around:
-        c.wait_recv()
-    for s, (n, peer, other) in enumerate(((1, next_z, rep_y), (0, next_y, rep_z))):
-        ref = piece(across_m, other, s)
-        c = send(ref, ref, yzsem.at[0, n, 2], yzsem.at[1, n, 2], peer)
-        c.start()
-        around.append(c)
-    for other in (rep_y, rep_z):
-        for s in range(2):
-            to_mate(piece(across_m, other, s))
     push_q1.wait()
     for j in range(chunks):
         hcopies[j].wait_recv()
@@ -254,9 +280,9 @@
         kvn[2 + n] = t.astype(BF16).astype(F32)
     for i in range(4):
         q_out[chip * 4 + i] = q1own[i, 0:rows, :]
-    for s in range(2):
-        around[4 + s].wait_recv()
-    for s in range(2):
+    for s in range(subs):
+        around[2 * subs + s].wait_recv()
+    for s in range(subs):
         to_mate(piece(across_m, rep_yz, s))
     for i in range(4):
         q1copies[i].wait_recv()
@@ -269,11 +295,26 @@
         c.wait()
 
 
+def write_out(bufs, ko, vo, layer, sems):
+    outs = []
+    for i in range(2):
+        for n, (src, dst) in enumerate(zip(bufs, (ko, vo))):
+            part = pl.ds(i * (src.shape[0] // 2), src.shape[0] // 2)
+            c = pltpu.make_async_copy(src.at[part], dst.at[layer, part], sems.at[n, i])
+            c.start()
+            outs.append(c)
+    return outs
+
+
+def write1_kernel(k1, v1, _k, _v, ko, vo, osem):
+    for c in write_out((k1, v1), ko, vo, 1, osem):
+        c.wait()
+
+
 def attend1_kernel(len_ref, q_ref, kvn, k0, v0, k1, v1, ctx, _k0, _v0, _k1, _v1, ko, vo, qs, st, osem):
     heads, rows, dim = q_ref.shape
     base = lax.axis_index("model") * rows
     tile = 16
-    outs = []
     for layer, bufs in enumerate(((k0, v0), (k1, v1))):
         def patch(b, carry):
             ln = len_ref[base + b]
@@ -285,12 +326,8 @@
             return carry
 
         lax.fori_loop(0, rows, patch, 0, unroll=4)
-        for i in range(2):
-            for n, (src, dst) in enumerate(zip(bufs, (ko, vo))):
-                part = pl.ds(i * (rows // 2), rows // 2)
-                c = pltpu.make_async_copy(src.at[part], dst.at[layer, part], osem.at[layer, n, i])
-                c.start()
-                outs.append(c)
+        if layer == 0:
+            outs = write_out(bufs, ko, vo, 0, osem)
     scatter_queries(lambda h: q_ref[h], qs, heads, rows)
     attend_rows(range(rows), heads, lambda b: len_ref[base + b], k1, v1, qs, st)
     gather_contexts(ctx, qs, 0, rows, heads)
@@ -298,20 +335,14 @@
         c.wait()
 
 
-def last_kernel(ctx, hid, wof, out, other, acc, hl, pl2, gsem, hsem, psem):
+def last_kernel(ctx, other, hid, wof, out, acc, hl, pl2, hsem, psem):
     rep, m, core, chip = place()
     across_m, mate_m = lax.rem(m + 2, 4), m + 1 - 2 * core
     across, mate = (rep, across_m), (rep, mate_m)
     heads, rows, dim = ctx.shape
     chunks = hl.shape[0]
     cols = chunks // 2
-    meet((across, mate))
-    gives = []
-    for p in range(4):
-        two = pl.ds(2 * p, 2)
-        c = send(ctx.at[two], other.at[two], gsem.at[0, p], gsem.at[1, p], across)
-        c.start()
-        gives.append(c)
+    greet((across, mate))
     hcopies = []
     pcopies = []
 
@@ -322,7 +353,6 @@
         pcopies.append(c)
 
     for p in range(4):
-        gives[p].wait_recv()
         left = [jnp.concatenate((ctx[2 * p + i], other[2 * p + i]), axis=0) for i in range(2)]
         for j in range(cols):
             part = dot(left[0], wof[2 * p, :, j * dim:(j + 1) * dim]) + dot(left[1], wof[2 * p + 1, :, j * dim:(j + 1) * dim])
@@ -332,6 +362,8 @@
                 acc[j] += part
             else:
                 at = chip * cols + j
+                if j == 0:
+                    meet((across, mate))
                 hl[at] = (hid[at].astype(F32) + (acc[j] + part)).astype(BF16)
                 for n in range(2):
                     c = send(hl.at[at, pl.ds(n * rows, rows)], hl.at[at, pl.ds((1 - n) * rows, rows)],
@@ -355,7 +387,7 @@
     for j in range(chunks):
         put(mate_m, j, pl2[j, 0:rows, :])
         put(3 - m, j, pl2[j, rows:2 * rows, :])
-    for c in gives + hcopies + pcopies:
+    for c in hcopies + pcopies:
         c.wait_send()
 
 
@@ -370,9 +402,9 @@
         local = w_query.shape[-1]
         heads = local // dim * mesh.shape["model"]
         hd = (heads, rows, dim)
-        x, w_query, w_key, w_value, w_out, k_cache, v_cache = (
+        x, cache_len, w_query, w_key, w_value, w_out, k_cache, v_cache = (
             pltpu.with_memory_space_constraint(a, pltpu.HBM)
-            for a in (x, w_query, w_key, w_value, w_out, k_cache, v_cache))
+            for a in (x, cache_len, w_query, w_key, w_value, w_out, k_cache, v_cache))
         remote = functools.partial(pltpu.CompilerParams, has_side_effects=True)
         cache = pltpu.VMEM((rows, seq, dim), BF16)
         qs = pltpu.VMEM((2, rows * heads, 128), F32)
@@ -394,37 +426,50 @@
                 pltpu.VMEM((4, 2 * rows, dim), F32), pltpu.VMEM((4, 2 * rows, dim), BF16),
                 pltpu.VMEM((4, rows, dim), BF16), pltpu.VMEM((local // 4, width // 2), BF16),
                 DMA((10,)), DMA((6, 8)), DMA((4,)), DMA((2, 3, 2)), DMA((2, 2)), DMA((2, 2)), DMA((2, chunks)), DMA((2, chunks)),
-                DMA((2, 4)), DMA((2, 2)), DMA((2, 2, 3)), DMA((2, 10)),
+                DMA((2, 4)), DMA((2, 4)), DMA((2, 2, 6)), DMA((2, 18)),
             ],
             compiler_params=remote(collective_id=0, vmem_limit_bytes=11 << 20),
             name="layer0",
         )(cache_len, x, w_query, w_key, w_value, w_out, k_cache, v_cache)
 
-        ctx, _, _, _, _, ko, vo = pl.pallas_call(
+        ctx, _, _, k1, v1, ko, vo = pl.pallas_call(
             attend1_kernel,
             out_shape=(pltpu.VMEM(hd, BF16), cache, cache, cache, cache,
                        jax.ShapeDtypeStruct(k_cache.shape, BF16), jax.ShapeDtypeStruct(v_cache.shape, BF16)),
             in_specs=[SM] + [VM] * 6,
             out_specs=(VM,) * 5 + (HBM, HBM),
             input_output_aliases={3: 1, 4: 2, 5: 3, 6: 4},
-            scratch_shapes=[qs, st, DMA((2, 2, 2))],
+            scratch_shapes=[qs, st, DMA((2, 2))],
             compiler_params=pltpu.CompilerParams(vmem_limit_bytes=3 << 20),
             name="attend1",
         )(cache_len, q, kvn, *caches)
 
+        other = lax.ppermute(ctx, "model", [(i, (i + 2) % 4) for i in range(4)])
+        ko, vo = pl.pallas_call(
+            write1_kernel,
+            out_shape=(jax.ShapeDtypeStruct(k_cache.shape, BF16), jax.ShapeDtypeStruct(v_cache.shape, BF16)),
+            in_specs=[VM, VM, HBM, HBM],
+            out_specs=(HBM, HBM),
+            input_output_aliases={2: 0, 3: 1},
+            scratch_shapes=[DMA((2, 2))],
+            compiler_params=pltpu.CompilerParams(vmem_limit_bytes=1 << 20),
+            cost_estimate=pl.CostEstimate(flops=10 ** 9, bytes_accessed=2 ** 25, transcendentals=0),
+            name="write1",
+        )(k1, v1, ko, vo)
+
         out = pl.pallas_call(
             last_kernel,
             out_shape=pltpu.VMEM((total, width), BF16),
-            in_specs=[VM] * 3,
+            in_specs=[VM] * 4,
             out_specs=VM,
             scratch_shapes=[
-                pltpu.VMEM(hd, BF16), pltpu.VMEM((chunks // 2, 2 * rows, dim), F32),
+                pltpu.VMEM((chunks // 2, 2 * rows, dim), F32),
                 pltpu.VMEM((chunks, 2 * rows, dim), BF16), pltpu.VMEM((chunks, 2 * rows, dim), BF16),
-                DMA((2, 4)), DMA((2, 2, chunks // 2)), DMA((2, chunks)),
+                DMA((2, 2, chunks // 2)), DMA((2, chunks)),
             ],
             compiler_params=remote(collective_id=1, vmem_limit_bytes=4 << 20),
             name="last",
-        )(ctx, hid, wof)
+        )(ctx, other, hid, wof)
         return out, ko, vo
 
     return jax.shard_map(

time: 60.5 us -> 55.1 us (0.911)
  Pallas kernels: 58.3 us -> 52.2 us
  starting transfers between devices: 0 us -> 1.25 us
  local copies, waits for them, and re-layouts: 1.44 us -> 0.8 us
    pallas_call x0 -> x1, Pallas kernels: none -> 5.95 us  [device_step(): pl.pallas_call(write1_kernel, out_shape=(jax.ShapeDtypeStruct(k_cache.sha...]
    pallas_call x1, Pallas kernels: 11.6 us -> 6.16 us  [device_step(): pl.pallas_call(last_kernel, out_shape=pltpu.VMEM((total, width), BF16), i...]
    pallas_call x1, Pallas kernels: 11.9 us -> 6.97 us  [device_step(): pl.pallas_call(attend1_kernel, out_shape=(pltpu.VMEM(hd, BF16), cache, ca...]
    pallas_call x1, Pallas kernels: 34.7 us -> 33.1 us  [device_step(): pl.pallas_call(layer0_kernel, out_shape=(pltpu.VMEM(hd, BF16), pltpu.VMEM...]
    ppermute x0 -> x1, starting transfers between devices: none -> 1.25 us  [device_step(): other = lax.ppermute(ctx, 'model', [(i, (i + 2) % 4) for i in range(4)])]
    unnamed x3 -> x1, local copies, waits for them, and re-layouts: 1.44 us -> 0.8 us
  transfers between devices with their start and end apart: 0 -> 1, of which waited for: 0 -> 0; matrix products, arithmetic and copies ran while one was open for 0% -> 0% of each run, Pallas kernels for 0% -> 11%
where the time goes in v4:
time: 55.1 us; the launch traced here: 54.9 us
  Pallas kernels  52.2 us (95%)
  starting transfers between devices  1.25 us (2%)
  local copies, waits for them, and re-layouts  0.8 us (1%)
  between operations  0.67 us (1%)
    pallas_call x1, Pallas kernels, device_step(): pl.pallas_call(layer0_kernel, out_shape=(pltpu.VMEM(hd, BF16), pltpu.VMEM...  33.1 us
    pallas_call x1, Pallas kernels, device_step(): pl.pallas_call(attend1_kernel, out_shape=(pltpu.VMEM(hd, BF16), cache, ca...  6.97 us
    pallas_call x1, Pallas kernels, device_step(): pl.pallas_call(last_kernel, out_shape=pltpu.VMEM((total, width), BF16), i...  6.16 us
    pallas_call x1, Pallas kernels, device_step(): pl.pallas_call(write1_kernel, out_shape=(jax.ShapeDtypeStruct(k_cache.sha...  5.95 us
    ppermute x1, starting transfers between devices, device_step(): other = lax.ppermute(ctx, 'model', [(i, (i + 2) % 4) for i in range(4)])  1.25 us
  transfers between devices with their start and end apart: 1, of which 0 were waited for; matrix products, arithmetic and copies ran while one was open for 0% of the time, Pallas kernels for 11%

profile of v4, /device:TPU:0, one launch (start us, length us, event | category | flops | bytes accessed | tf_op | source)
XLA Modules:
  0.0 54.9 jit_solution(13773867597219355131)
XLA Ops:
  0.6 33.1 %layer0.1 = (bf16[8,32,256]{2,1,0:T(8,128)(2,1)S(1)}, f32[4,32,256]{2,1,0:T(8,128)S(1)}, bf16[8,64,256]{2,1,0:T(8,128)(2,1)S(1)}, bf16[8,256,1024]{2,1,0:T(8,128...) custom-call(s32[128]{0:T(128)} %len_ref.3, ...), custom_call_target="tpu_custom_call" | custom-call | tf_op jit(solution)/shard_map/layer0/pallas_call | solution.py:413
  33.8 7.0 %attend1.1 = (bf16[8,32,256]{2,1,0:T(8,128)(2,1)S(1)}, bf16[32,512,256]{2,1,0:T(8,128)(2,1)S(1)}, bf16[32,512,256]{2,1,0:T(8,128)(2,1)S(1)}, bf16[32,512,256]{2,...) custom-call(s32[128]{0:T(128)} %len_ref.3, ...), custom_call_target="tpu_custom_call", output_to_operand_aliasing={{1}: (3, {}), {2}: (4, {}), {3}: (5, {}), {4}: (6, {})} | custom-call | tf_op jit(solution)/shard_map/attend1/pallas_call | solution.py:435
  40.8 1.3 %collective-permute-start = (bf16[8,32,256]{2,1,0:T(8,128)(2,1)S(1)}, bf16[8,32,256]{2,1,0:T(8,128)(2,1)S(1)}, u32[]{:S(2)}, u32[]{:S(2)}) collective-permute-start(bf16[8,32,256]{2,1,0:T(8,128)(2,1)S(1)} %get-tuple-element.24.ctx), channel_id=1, source_target_pairs={{0,2},{1,3},{2,0},{3,1},{4,6},{5,7},{6,4},{7,5},{8,10},{9,11},{10,... | collective-permute-start | bytes 393224 | tf_op jit(solution)/shard_map/ppermute | solution.py:447
  42.0 5.9 %write1.1 = (bf16[2,32,512,256]{3,2,1,0:T(8,128)(2,1)}, bf16[2,32,512,256]{3,2,1,0:T(8,128)(2,1)}) custom-call(bf16[32,512,256]{2,1,0:T(8,128)(2,1)S(1)} %get-tuple-element.27.k1, bf16[32,512,256]{2,1,0:T(8,128)(2,1)S(1)} %get-tuple-element.28.v1, bf16[2,32,512,256]{3,2,1,0:T(8,128)(2,1)} %get-tuple-element.29._k, ...), custom_call_target="tpu_custom_call", output_to_operand_aliasing={{0}: (2, {}), {1}: (3, {})} | custom-call | flops 1000000000 | bytes 33554432 | tf_op jit(solution)/shard_map/write1/pallas_call | solution.py:448
  48.0 0.0 collective-permute-done.other
  48.0 6.2 %last.1 = bf16[128,2048]{1,0:T(8,128)(2,1)S(1)} custom-call(bf16[8,32,256]{2,1,0:T(8,128)(2,1)S(1)} %get-tuple-element.24.ctx, bf16[8,32,256]{2,1,0:T(8,128)(2,1)S(1)} %collective-permute-done.other, bf16[8,64,256]{2,1,0:T(8,128)(2,1)S(1)} %get-tuple-element.25.hid, bf16[8,256,1024]{2,1,0:T(8,128)(2,1)S(1)} %get-tuple-element.26.wof), custom_call_target="tpu_custom_call" | custom-call | tf_op jit(solution)/shard_map/last/pallas_call | solution.py:460
  54.1 0.8 %copy.24 = bf16[128,2048]{1,0:T(8,128)(2,1)} copy(bf16[128,2048]{1,0:T(8,128)(2,1)S(1)} %last.1) | data formatting | bytes 1048576
Async XLA Ops:
  40.8 7.2 %collective-permute-start = (bf16[8,32,256]{2,1,0:T(8,128)(2,1)S(1)}, bf16[8,32,256]{2,1,0:T(8,128)(2,1)S(1)}, u32[]{:S(2)}, u32[]{:S(2)}) collective-permute-start(bf16[8,32,256]{2,1,0:T(8,128)(2,1)S(1)} %get-tuple-element.24.ctx), channel_id=1, source_target_pairs={{0,2},{1,3},{2,0},{3,1},{4,6},{5,7},{6,4},{7,5},{8,10},{9,11},{10,... | collective-permute-start | bytes 393224 | tf_op jit(solution)/shard_map/ppermute | solution.py:447

commit v5 on v4

--- a/solution.py
+++ b/solution.py
@@ -87,12 +87,12 @@
 def layer0_kernel(len_ref, x_hbm, wq_hbm, wk_hbm, wv_hbm, wo_hbm, kc_hbm, vc_hbm,
                   q_out, kvn, hl, wof, k0, v0, k1, v1,
                   xs, qown, qrecv, qs, ctx, wos, lhs, ys, yrecv, wq1, qacc, q1own, q1recv, stage,
-                  wsem, lsem, csem, qsem, gsem, psem, ysem, hsem, q1sem, xsem, yzsem, msem):
+                  wsem, lsem, c0sem, csem, qsem, gsem, psem, ysem, hsem, q1sem, xsem, yzsem, msem):
     rep, m, core, chip = place()
     heads, rows, dim = q_out.shape
     half = rows // 2
     chunks = hl.shape[0]
-    across_m, mate_m, diag_m = lax.rem(m + 2, 4), m + 1 - 2 * core, 3 - m
+    across_m, mate_m, diag_m = 3 - m, m + 1 - 2 * core, lax.rem(m + 2, 4)
     across, mate, diag = (rep, across_m), (rep, mate_m), (rep, diag_m)
     rep_y, rep_z, rep_yz = rep + 1 - 2 * lax.rem(rep, 2), lax.rem(rep + 2, 4), 3 - rep
     next_y, next_z = (rep_y, m), (rep_z, m)
@@ -115,6 +115,14 @@
         xcopies.append(c)
 
     around = []
+
+    mcopies = []
+
+    def to_mate(ref):
+        n = len(mcopies)
+        c = send(ref, ref, msem.at[0, n], msem.at[1, n], mate)
+        c.start()
+        mcopies.append(c)
 
     def pass_round(s):
         xcopies[s].wait_recv()
@@ -141,8 +149,9 @@
 
     def first_weights(n, rows_ref):
         total = None
+        for c in loads[n]:
+            c.wait()
         for t in range(blocks):
-            loads[n][t].wait()
             part = dot(rows_ref[:, t * deep:(t + 1) * deep], k1[n * blocks + t])
             total = part if t == 0 else total + part
         return total.astype(BF16)
@@ -152,14 +161,16 @@
     load_stage = pltpu.make_async_copy(
         wo_hbm.at[1, pl.ds(pl.multiple_of(rep * quarter, quarter), quarter), theirs], stage, wsem.at[5])
     load_stage.start()
-    loads0 = [pltpu.make_async_copy(kc_hbm.at[0], k0, csem.at[0]), pltpu.make_async_copy(vc_hbm.at[0], v0, csem.at[1])]
+    groups = [pl.ds(g * half, half) for g in range(2)]
+    loads0 = [[pltpu.make_async_copy(src.at[0, groups[g]], dst.at[groups[g]], c0sem.at[g, n])
+               for n, (src, dst) in enumerate(((kc_hbm, k0), (vc_hbm, v0)))] for g in range(2)]
     load_x.wait()
     start(loads[2] + loads[3])
     qcopies = []
     for i in range(2):
         q = first_weights(i, xs)
         if i == 0:
-            start(loads0[:1])
+            start(loads0[0])
             meet(friends)
             load_stage.wait()
         for d in range(4):
@@ -173,7 +184,7 @@
     load_q1 = pltpu.make_async_copy(wq_hbm.at[1], wq1.at[core], wsem.at[7])
     load_own = [pltpu.make_async_copy(wo_hbm.at[1, pl.ds(i * dim, dim), ours], wof.at[2 * m + i], wsem.at[8 + i])
                 for i in range(2)]
-    start(loads0[1:])
+    start([load_wo] + loads0[1])
     for s in range(subs):
         send_quarter(s)
     mine = xs[pl.ds(pl.multiple_of(m * rows, rows), rows), :]
@@ -182,62 +193,56 @@
     for c in qcopies:
         c.wait()
     scatter_queries(lambda h: qrecv[h // 2, h % 2], qs, heads, rows)
-    loads0[0].wait()
-    start([load_wo, load_q1] + load_own)
-    loads1 = [pltpu.make_async_copy(kc_hbm.at[1], k1, csem.at[2]), pltpu.make_async_copy(vc_hbm.at[1], v1, csem.at[3])]
+    loads1 = [pltpu.make_async_copy(kc_hbm.at[1], k1, csem.at[0]), pltpu.make_async_copy(vc_hbm.at[1], v1, csem.at[1])]
     base = m * rows
-    pass_round(0)
     gives = []
     for g in range(2):
+        loads0[g][0].wait()
         attend_rows(range(g * half, (g + 1) * half), heads, lambda b: len_ref[base + b], k0, v0, qs, ys,
-                    (kvn.at[0], kvn.at[1]), loads0[1] if g == 0 else None)
+                    (kvn.at[0], kvn.at[1]), loads0[g][1])
         gather_contexts(ctx, qs, g * half, half, heads)
         c = send(ctx.at[pl.ds((1 - chip) * 4, 4), pl.ds(g * half, half), :],
-                 lhs.at[:, pl.ds(rows + g * half, half), :], gsem.at[0, g], gsem.at[1, g], across)
+                 lhs.at[:, pl.ds(g * rows + half, half), :], gsem.at[0, g], gsem.at[1, g], across)
         c.start()
         gives.append(c)
         if g == 0:
-            start(loads1)
+            start([load_q1] + load_own)
             load_wo.wait()
             push_wo = send(wos.at[core], wos.at[core], psem.at[0, 0], psem.at[1, 0], mate)
             push_wo.start()
-            load_q1.wait()
-            push_q1 = send(wq1.at[core], wq1.at[core], psem.at[0, 1], psem.at[1, 1], mate)
-            push_q1.start()
-            pass_round(1)
-    for i in range(4):
-        lhs[i, 0:rows, :] = ctx[chip * 4 + i]
-    mcopies = []
-
-    def to_mate(ref):
-        n = len(mcopies)
-        c = send(ref, ref, msem.at[0, n], msem.at[1, n], mate)
-        c.start()
-        mcopies.append(c)
-
-    for s in range(2, subs):
+            pass_round(0)
+    load_q1.wait()
+    push_q1 = send(wq1.at[core], wq1.at[core], psem.at[0, 1], psem.at[1, 1], mate)
+    push_q1.start()
+    for i in range(2):
+        load_own[i].wait()
+        to_mate(wof.at[2 * m + i])
+    start(loads1)
+    to_mate(piece(across_m, rep, 0))
+    for s in range(1, subs):
         pass_round(s)
+        to_mate(piece(across_m, rep, s))
+    for g in range(2):
+        for i in range(4):
+            lhs[i, g * rows:g * rows + half, :] = ctx[chip * 4 + i, g * half:(g + 1) * half, :]
     push_wo.wait()
-    for c in gives:
-        c.wait()
     ycopies = []
-    for j in range(chunks):
-        y = dot(lhs[0], wos[0, 0:256, j * 256:(j + 1) * 256])
-        for i in range(1, 4):
-            y += dot(lhs[i], wos[i // 2, (i % 2) * 256:(i % 2 + 1) * 256, j * 256:(j + 1) * 256])
-        ys[j] = y
-        c = send(ys.at[j, pl.ds(rows, rows)], yrecv.at[j], ysem.at[0, j], ysem.at[1, j], across)
-        c.start()
-        ycopies.append(c)
+    for g in range(2):
+        gives[g].wait()
+        both = slice(g * rows, (g + 1) * rows)
+        for j in range(chunks):
+            y = dot(lhs[0, both, :], wos[0, 0:256, j * 256:(j + 1) * 256])
+            for i in range(1, 4):
+                y += dot(lhs[i, both, :], wos[i // 2, (i % 2) * 256:(i % 2 + 1) * 256, j * 256:(j + 1) * 256])
+            ys[j, both, :] = y
+            n = g * chunks + j
+            c = send(ys.at[j, pl.ds(g * rows + half, half)], yrecv.at[j, pl.ds(g * half, half)], ysem.at[0, n], ysem.at[1, n], across)
+            c.start()
+            ycopies.append(c)
     loads_kv = [[pltpu.make_async_copy(src.at[1, pl.ds(j * dim, dim)], wos.at[0, pl.ds(n * dim, dim), pl.ds(j * dim, dim)],
                                        lsem.at[4 + n, j]) for j in range(chunks)] for n, src in enumerate((wk_hbm, wv_hbm))]
     for c in loads_kv[0] + loads_kv[1]:
         c.start()
-    for i in range(2):
-        load_own[i].wait()
-        to_mate(wof.at[2 * m + i])
-    for s in range(subs):
-        to_mate(piece(across_m, rep, s))
     for c in around:
         c.wait_recv()
     for s in range(subs):
@@ -250,16 +255,20 @@
         for s in range(subs):
             to_mate(piece(across_m, other, s))
     hcopies = []
-    for j in range(chunks):
-        ycopies[j].wait_recv()
-        old = xs[pl.ds(pl.multiple_of(m * rows, rows), rows), j * 256:(j + 1) * 256]
-        hl[j, 0:rows, :] = (old.astype(F32) + (ys[j, 0:rows, :] + yrecv[j])).astype(BF16)
-        c = send(hl.at[j, pl.ds(0, rows)], hl.at[j, pl.ds(rows, rows)], hsem.at[0, j], hsem.at[1, j], across)
-        c.start()
-        hcopies.append(c)
+    for g in range(2):
+        for j in range(chunks):
+            n = g * chunks + j
+            ycopies[n].wait_recv()
+            part = slice(g * half, (g + 1) * half)
+            old = xs[pl.ds(pl.multiple_of(m * rows + g * half, half), half), j * 256:(j + 1) * 256]
+            hl[j, part, :] = (old.astype(F32) + (ys[j, g * rows:g * rows + half, :] + yrecv[j, part, :])).astype(BF16)
+            c = send(hl.at[j, pl.ds(g * half, half)], hl.at[j, pl.ds(rows + g * half, half)], hsem.at[0, n], hsem.at[1, n], across)
+            c.start()
+            hcopies.append(c)
     push_q1.wait()
     for j in range(chunks):
-        hcopies[j].wait_recv()
+        for g in range(2):
+            hcopies[g * chunks + j].wait_recv()
         for i in range(4):
             part = dot(hl[j], wq1[i // 2, j * 256:(j + 1) * 256, (i % 2) * 256:(i % 2 + 1) * 256])
             if j == 0:
@@ -335,9 +344,9 @@
         c.wait()
 
 
-def last_kernel(ctx, other, hid, wof, out, acc, hl, pl2, hsem, psem):
+def last_kernel(ctx, other, hid, wof, out, left, hl, pl2, hsem, psem):
     rep, m, core, chip = place()
-    across_m, mate_m = lax.rem(m + 2, 4), m + 1 - 2 * core
+    across_m, mate_m, diag_m = 3 - m, m + 1 - 2 * core, lax.rem(m + 2, 4)
     across, mate = (rep, across_m), (rep, mate_m)
     heads, rows, dim = ctx.shape
     chunks = hl.shape[0]
@@ -352,25 +361,23 @@
         c.start()
         pcopies.append(c)
 
-    for p in range(4):
-        left = [jnp.concatenate((ctx[2 * p + i], other[2 * p + i]), axis=0) for i in range(2)]
-        for j in range(cols):
-            part = dot(left[0], wof[2 * p, :, j * dim:(j + 1) * dim]) + dot(left[1], wof[2 * p + 1, :, j * dim:(j + 1) * dim])
-            if p == 0:
-                acc[j] = part
-            elif p < 3:
-                acc[j] += part
-            else:
-                at = chip * cols + j
-                if j == 0:
-                    meet((across, mate))
-                hl[at] = (hid[at].astype(F32) + (acc[j] + part)).astype(BF16)
-                for n in range(2):
-                    c = send(hl.at[at, pl.ds(n * rows, rows)], hl.at[at, pl.ds((1 - n) * rows, rows)],
-                             hsem.at[0, n, j], hsem.at[1, n, j], across)
-                    c.start()
-                    hcopies.append(c)
-                to_mate(at)
+    for h in range(heads):
+        left[h, 0:rows, :] = ctx[h]
+        left[h, rows:2 * rows, :] = other[h]
+    for j in range(cols):
+        y = dot(left[0], wof[0, :, j * dim:(j + 1) * dim])
+        for h in range(1, heads):
+            y += dot(left[h], wof[h, :, j * dim:(j + 1) * dim])
+        at = chip * cols + j
+        hl[at] = (hid[at].astype(F32) + y).astype(BF16)
+        if j == 0:
+            meet((across, mate))
+        for n in range(2):
+            c = send(hl.at[at, pl.ds(n * rows, rows)], hl.at[at, pl.ds((1 - n) * rows, rows)],
+                     hsem.at[0, n, j], hsem.at[1, n, j], across)
+            c.start()
+            hcopies.append(c)
+        to_mate(at)
     for j in range(cols):
         for n in range(2):
             hcopies[2 * j + n].wait_recv()
@@ -386,7 +393,7 @@
         c.wait_recv()
     for j in range(chunks):
         put(mate_m, j, pl2[j, 0:rows, :])
-        put(3 - m, j, pl2[j, rows:2 * rows, :])
+        put(diag_m, j, pl2[j, rows:2 * rows, :])
     for c in hcopies + pcopies:
         c.wait_send()
 
@@ -425,7 +432,7 @@
                 pltpu.VMEM((2, width, local), BF16),
                 pltpu.VMEM((4, 2 * rows, dim), F32), pltpu.VMEM((4, 2 * rows, dim), BF16),
                 pltpu.VMEM((4, rows, dim), BF16), pltpu.VMEM((local // 4, width // 2), BF16),
-                DMA((10,)), DMA((6, 8)), DMA((4,)), DMA((2, 3, 2)), DMA((2, 2)), DMA((2, 2)), DMA((2, chunks)), DMA((2, chunks)),
+                DMA((10,)), DMA((6, 8)), DMA((2, 2)), DMA((2,)), DMA((2, 3, 2)), DMA((2, 2)), DMA((2, 2)), DMA((2, 2 * chunks)), DMA((2, 2 * chunks)),
                 DMA((2, 4)), DMA((2, 4)), DMA((2, 2, 6)), DMA((2, 18)),
             ],
             compiler_params=remote(collective_id=0, vmem_limit_bytes=11 << 20),
@@ -444,7 +451,7 @@
             name="attend1",
         )(cache_len, q, kvn, *caches)
 
-        other = lax.ppermute(ctx, "model", [(i, (i + 2) % 4) for i in range(4)])
+        other = lax.ppermute(ctx, "model", [(i, 3 - i) for i in range(4)])
         ko, vo = pl.pallas_call(
             write1_kernel,
             out_shape=(jax.ShapeDtypeStruct(k_cache.shape, BF16), jax.ShapeDtypeStruct(v_cache.shape, BF16)),
@@ -463,7 +470,7 @@
             in_specs=[VM] * 4,
             out_specs=VM,
             scratch_shapes=[
-                pltpu.VMEM((chunks // 2, 2 * rows, dim), F32),
+                pltpu.VMEM((heads, 2 * rows, dim), BF16),
                 pltpu.VMEM((chunks, 2 * rows, dim), BF16), pltpu.VMEM((chunks, 2 * rows, dim), BF16),
                 DMA((2, 2, chunks // 2)), DMA((2, chunks)),
             ],

time: 55.1 us -> 53 us (0.962)
  Pallas kernels: 52.2 us -> 51.1 us
  starting transfers between devices: 1.25 us -> 0.25 us
    pallas_call x1, Pallas kernels: 33.1 us -> 31.3 us  [device_step(): pl.pallas_call(layer0_kernel, out_shape=(pltpu.VMEM(hd, BF16), pltpu.VMEM...]
    ppermute x1, starting transfers between devices: 1.25 us -> 0.25 us  [device_step(): other = lax.ppermute(ctx, 'model', [(i, 3 - i) for i in range(4)])]
    pallas_call x1, Pallas kernels: 6.16 us -> 6.91 us  [device_step(): pl.pallas_call(last_kernel, out_shape=pltpu.VMEM((total, width), BF16), i...]
where the time goes in v5:
time: 53 us; the launch traced here: 52.8 us
  Pallas kernels  51.1 us (96%)
  local copies, waits for them, and re-layouts  0.8 us (2%)
  between operations  0.67 us (1%)
    pallas_call x1, Pallas kernels, device_step(): pl.pallas_call(layer0_kernel, out_shape=(pltpu.VMEM(hd, BF16), pltpu.VMEM...  31.3 us
    pallas_call x1, Pallas kernels, device_step(): pl.pallas_call(attend1_kernel, out_shape=(pltpu.VMEM(hd, BF16), cache, ca...  6.97 us
    pallas_call x1, Pallas kernels, device_step(): pl.pallas_call(last_kernel, out_shape=pltpu.VMEM((total, width), BF16), i...  6.91 us
    pallas_call x1, Pallas kernels, device_step(): pl.pallas_call(write1_kernel, out_shape=(jax.ShapeDtypeStruct(k_cache.sha...  5.95 us
  transfers between devices with their start and end apart: 1, of which 0 were waited for; matrix products, arithmetic and copies ran while one was open for 0% of the time, Pallas kernels for 11%

profile of v5, /device:TPU:0, one launch (start us, length us, event | category | flops | bytes accessed | tf_op | source)
XLA Modules:
  0.0 52.8 jit_solution(1841920009261067313)
XLA Ops:
  0.6 31.3 %layer0.1 = (bf16[8,32,256]{2,1,0:T(8,128)(2,1)S(1)}, f32[4,32,256]{2,1,0:T(8,128)S(1)}, bf16[8,64,256]{2,1,0:T(8,128)(2,1)S(1)}, bf16[8,256,1024]{2,1,0:T(8,128...) custom-call(s32[128]{0:T(128)} %len_ref.3, ...), custom_call_target="tpu_custom_call" | custom-call | tf_op jit(solution)/shard_map/layer0/pallas_call | solution.py:420
  31.9 7.0 %attend1.1 = (bf16[8,32,256]{2,1,0:T(8,128)(2,1)S(1)}, bf16[32,512,256]{2,1,0:T(8,128)(2,1)S(1)}, bf16[32,512,256]{2,1,0:T(8,128)(2,1)S(1)}, bf16[32,512,256]{2,...) custom-call(s32[128]{0:T(128)} %len_ref.3, ...), custom_call_target="tpu_custom_call", output_to_operand_aliasing={{1}: (3, {}), {2}: (4, {}), {3}: (5, {}), {4}: (6, {})} | custom-call | tf_op jit(solution)/shard_map/attend1/pallas_call | solution.py:442
  38.9 0.3 collective-permute-start
  39.2 5.9 %write1.1 = (bf16[2,32,512,256]{3,2,1,0:T(8,128)(2,1)}, bf16[2,32,512,256]{3,2,1,0:T(8,128)(2,1)}) custom-call(bf16[32,512,256]{2,1,0:T(8,128)(2,1)S(1)} %get-tuple-element.27.k1, bf16[32,512,256]{2,1,0:T(8,128)(2,1)S(1)} %get-tuple-element.28.v1, bf16[2,32,512,256]{3,2,1,0:T(8,128)(2,1)} %get-tuple-element.29._k, ...), custom_call_target="tpu_custom_call", output_to_operand_aliasing={{0}: (2, {}), {1}: (3, {})} | custom-call | flops 1000000000 | bytes 33554432 | tf_op jit(solution)/shard_map/write1/pallas_call | solution.py:455
  45.1 0.0 collective-permute-done.other
  45.1 6.9 %last.1 = bf16[128,2048]{1,0:T(8,128)(2,1)S(1)} custom-call(bf16[8,32,256]{2,1,0:T(8,128)(2,1)S(1)} %get-tuple-element.24.ctx, bf16[8,32,256]{2,1,0:T(8,128)(2,1)S(1)} %collective-permute-done.other, bf16[8,64,256]{2,1,0:T(8,128)(2,1)S(1)} %get-tuple-element.25.hid, bf16[8,256,1024]{2,1,0:T(8,128)(2,1)S(1)} %get-tuple-element.26.wof), custom_call_target="tpu_custom_call" | custom-call | tf_op jit(solution)/shard_map/last/pallas_call | solution.py:467
  52.0 0.8 %copy.24 = bf16[128,2048]{1,0:T(8,128)(2,1)} copy(bf16[128,2048]{1,0:T(8,128)(2,1)S(1)} %last.1) | data formatting | bytes 1048576
Async XLA Ops:
  38.9 6.2 %collective-permute-start = (bf16[8,32,256]{2,1,0:T(8,128)(2,1)S(1)}, bf16[8,32,256]{2,1,0:T(8,128)(2,1)S(1)}, u32[]{:S(2)}, u32[]{:S(2)}) collective-permute-start(bf16[8,32,256]{2,1,0:T(8,128)(2,1)S(1)} %get-tuple-element.24.ctx), channel_id=1, source_target_pairs={{0,3},{1,2},{2,1},{3,0},{4,7},{5,6},{6,5},{7,4},{8,11},{9,10},{10,... | collective-permute-start | bytes 393224 | tf_op jit(solution)/shard_map/ppermute | solution.py:454

commit v6 on v5

--- a/solution.py
+++ b/solution.py
@@ -40,30 +40,34 @@
         src_ref=src, dst_ref=dst, send_sem=send_sem, recv_sem=recv_sem, device_id=peer, device_id_type=MESH)
 
 
+LAG = 8
+
+
 def scatter_queries(get, qs, heads, rows):
     for h in range(heads):
         for i in range(2):
             qs[i, pl.ds(h, rows, stride=heads), :] = get(h)[:, i * 128:(i + 1) * 128].astype(F32)
 
 
-def attend_rows(which, heads, length, kb, vb, qs, st, new=None, values=None):
+def attend_rows(which, heads, length, kb, vb, qs, new=None):
     seq, dim = kb.shape[1:]
     scale = dim ** -0.5
     pos = lax.broadcasted_iota(jnp.int32, (heads, seq), 1)
-    for b in which:
+    waiting = []
+    for b in list(which) + [None] * LAG:
+        if b is not None:
+            cut = slice(b * heads, (b + 1) * heads)
+            q = jnp.concatenate([qs[i, cut, :] for i in range(2)], axis=1)
+            s = lax.dot_general(q.astype(BF16), kb[b], (((1,), (1,)), ((), ())), preferred_element_type=F32)
+            if new is not None:
+                s = jnp.where(pos == length(b), jnp.sum(q * new[0][b:b + 1, :], axis=1, keepdims=True), s)
+            waiting.append((b, jnp.where(pos <= length(b), s * scale, -jnp.inf)))
+        if b is not None and len(waiting) <= LAG:
+            continue
+        if not waiting:
+            continue
+        b, s = waiting.pop(0)
         cut = slice(b * heads, (b + 1) * heads)
-        q = jnp.concatenate([qs[i, cut, :] for i in range(2)], axis=1)
-        s = lax.dot_general(q.astype(BF16), kb[b], (((1,), (1,)), ((), ())), preferred_element_type=F32)
-        if new is not None:
-            s = jnp.where(pos == length(b), jnp.sum(q * new[0][b:b + 1, :], axis=1, keepdims=True), s)
-        s = jnp.where(pos <= length(b), s * scale, -jnp.inf)
-        for i in range(2):
-            st[4 * i + b // 8, b % 8 * heads:(b % 8 + 1) * heads, :] = s[:, i * 256:(i + 1) * 256]
-    if values is not None:
-        values.wait()
-    for b in which:
-        cut = slice(b * heads, (b + 1) * heads)
-        s = jnp.concatenate([st[4 * i + b // 8, b % 8 * heads:(b % 8 + 1) * heads, :] for i in range(2)], axis=1)
         e = jnp.exp(s - jnp.max(s, axis=1, keepdims=True))
         p = (e * (1.0 / jnp.sum(e, axis=1, keepdims=True))).astype(BF16)
         if new is None:
@@ -164,13 +168,14 @@
     groups = [pl.ds(g * half, half) for g in range(2)]
     loads0 = [[pltpu.make_async_copy(src.at[0, groups[g]], dst.at[groups[g]], c0sem.at[g, n])
                for n, (src, dst) in enumerate(((kc_hbm, k0), (vc_hbm, v0)))] for g in range(2)]
+    load_wo = pltpu.make_async_copy(wo_hbm.at[0], wos.at[core], wsem.at[6])
     load_x.wait()
-    start(loads[2] + loads[3])
+    start(loads[2] + loads[3] + loads0[0])
     qcopies = []
     for i in range(2):
         q = first_weights(i, xs)
         if i == 0:
-            start(loads0[0])
+            start([load_wo] + loads0[1])
             meet(friends)
             load_stage.wait()
         for d in range(4):
@@ -180,11 +185,9 @@
             c.start()
             qcopies.append(c)
         qrecv[m, i] = qown[m, i]
-    load_wo = pltpu.make_async_copy(wo_hbm.at[0], wos.at[core], wsem.at[6])
     load_q1 = pltpu.make_async_copy(wq_hbm.at[1], wq1.at[core], wsem.at[7])
     load_own = [pltpu.make_async_copy(wo_hbm.at[1, pl.ds(i * dim, dim), ours], wof.at[2 * m + i], wsem.at[8 + i])
                 for i in range(2)]
-    start([load_wo] + loads0[1])
     for s in range(subs):
         send_quarter(s)
     mine = xs[pl.ds(pl.multiple_of(m * rows, rows), rows), :]
@@ -197,9 +200,9 @@
     base = m * rows
     gives = []
     for g in range(2):
-        loads0[g][0].wait()
-        attend_rows(range(g * half, (g + 1) * half), heads, lambda b: len_ref[base + b], k0, v0, qs, ys,
-                    (kvn.at[0], kvn.at[1]), loads0[g][1])
+        for c in loads0[g]:
+            c.wait()
+        attend_rows(range(g * half, (g + 1) * half), heads, lambda b: len_ref[base + b], k0, v0, qs, (kvn.at[0], kvn.at[1]))
         gather_contexts(ctx, qs, g * half, half, heads)
         c = send(ctx.at[pl.ds((1 - chip) * 4, 4), pl.ds(g * half, half), :],
                  lhs.at[:, pl.ds(g * rows + half, half), :], gsem.at[0, g], gsem.at[1, g], across)
@@ -304,41 +307,44 @@
         c.wait()
 
 
-def write_out(bufs, ko, vo, layer, sems):
-    outs = []
-    for i in range(2):
-        for n, (src, dst) in enumerate(zip(bufs, (ko, vo))):
-            part = pl.ds(i * (src.shape[0] // 2), src.shape[0] // 2)
-            c = pltpu.make_async_copy(src.at[part], dst.at[layer, part], sems.at[n, i])
-            c.start()
-            outs.append(c)
-    return outs
+PARTS = 4
+
+
+def write_out(buf, out, layer, sems):
+    copies = []
+    count = buf.shape[0] // PARTS
+    for i in range(PARTS):
+        part = pl.ds(i * count, count)
+        c = pltpu.make_async_copy(buf.at[part], out.at[layer, part], sems.at[i])
+        c.start()
+        copies.append(c)
+    return copies
 
 
 def write1_kernel(k1, v1, _k, _v, ko, vo, osem):
-    for c in write_out((k1, v1), ko, vo, 1, osem):
+    for c in write_out(k1, ko, 1, osem.at[0]) + write_out(v1, vo, 1, osem.at[1]):
         c.wait()
 
 
-def attend1_kernel(len_ref, q_ref, kvn, k0, v0, k1, v1, ctx, _k0, _v0, _k1, _v1, ko, vo, qs, st, osem):
+def attend1_kernel(len_ref, q_ref, kvn, k0, v0, k1, v1, ctx, _k0, _v0, _k1, _v1, ko, vo, qs, osem):
     heads, rows, dim = q_ref.shape
     base = lax.axis_index("model") * rows
     tile = 16
-    for layer, bufs in enumerate(((k0, v0), (k1, v1))):
+    outs = []
+    for n, buf in enumerate((k0, v0, k1, v1)):
         def patch(b, carry):
             ln = len_ref[base + b]
             start = pl.multiple_of((ln // tile) * tile, tile)
             hit = lax.broadcasted_iota(jnp.int32, (tile, dim), 0) == ln - start
-            for n, buf in enumerate(bufs):
-                old = buf[b, pl.ds(start, tile), :].astype(F32)
-                buf[b, pl.ds(start, tile), :] = jnp.where(hit, kvn[2 * layer + n, pl.ds(b, 1), :], old).astype(BF16)
+            old = buf[b, pl.ds(start, tile), :].astype(F32)
+            buf[b, pl.ds(start, tile), :] = jnp.where(hit, kvn[n, pl.ds(b, 1), :], old).astype(BF16)
             return carry
 
-        lax.fori_loop(0, rows, patch, 0, unroll=4)
-        if layer == 0:
-            outs = write_out(bufs, ko, vo, 0, osem)
+        lax.fori_loop(0, rows, patch, 0, unroll=8)
+        if n < 2:
+            outs += write_out(buf, (ko, vo)[n], 0, osem.at[n])
     scatter_queries(lambda h: q_ref[h], qs, heads, rows)
-    attend_rows(range(rows), heads, lambda b: len_ref[base + b], k1, v1, qs, st)
+    attend_rows(range(rows), heads, lambda b: len_ref[base + b], k1, v1, qs)
     gather_contexts(ctx, qs, 0, rows, heads)
     for c in outs:
         c.wait()
@@ -415,7 +421,6 @@
         remote = functools.partial(pltpu.CompilerParams, has_side_effects=True)
         cache = pltpu.VMEM((rows, seq, dim), BF16)
         qs = pltpu.VMEM((2, rows * heads, 128), F32)
-        st = pltpu.VMEM((chunks, 2 * rows, dim), F32)
 
         q, kvn, hid, wof, *caches = pl.pallas_call(
             layer0_kernel,
@@ -446,7 +451,7 @@
             in_specs=[SM] + [VM] * 6,
             out_specs=(VM,) * 5 + (HBM, HBM),
             input_output_aliases={3: 1, 4: 2, 5: 3, 6: 4},
-            scratch_shapes=[qs, st, DMA((2, 2))],
+            scratch_shapes=[qs, DMA((2, PARTS))],
             compiler_params=pltpu.CompilerParams(vmem_limit_bytes=3 << 20),
             name="attend1",
         )(cache_len, q, kvn, *caches)
@@ -458,7 +463,7 @@
             in_specs=[VM, VM, HBM, HBM],
             out_specs=(HBM, HBM),
             input_output_aliases={2: 0, 3: 1},
-            scratch_shapes=[DMA((2, 2))],
+            scratch_shapes=[DMA((2, PARTS))],
             compiler_params=pltpu.CompilerParams(vmem_limit_bytes=1 << 20),
             cost_estimate=pl.CostEstimate(flops=10 ** 9, bytes_accessed=2 ** 25, transcendentals=0),
             name="write1",

time: 53 us -> 52.5 us (level)
  no operation moved by 1% of the time
where the time goes in v6:
time: 52.5 us; the launch traced here: 52.4 us
  Pallas kernels  50.6 us (96%)
  local copies, waits for them, and re-layouts  0.8 us (2%)
  between operations  0.67 us (1%)
    pallas_call x1, Pallas kernels, device_step(): pl.pallas_call(layer0_kernel, out_shape=(pltpu.VMEM(hd, BF16), pltpu.VMEM...  31 us
    pallas_call x1, Pallas kernels, device_step(): pl.pallas_call(attend1_kernel, out_shape=(pltpu.VMEM(hd, BF16), cache, ca...  6.89 us
    pallas_call x1, Pallas kernels, device_step(): pl.pallas_call(last_kernel, out_shape=pltpu.VMEM((total, width), BF16), i...  6.82 us
    pallas_call x1, Pallas kernels, device_step(): pl.pallas_call(write1_kernel, out_shape=(jax.ShapeDtypeStruct(k_cache.sha...  5.92 us
  transfers between devices with their start and end apart: 1, of which 0 were waited for; matrix products, arithmetic and copies ran while one was open for 0% of the time, Pallas kernels for 11%

profile of v6, /device:TPU:0, one launch (start us, length us, event | category | flops | bytes accessed | tf_op | source)
XLA Modules:
  0.0 52.4 jit_solution(10700958850118851390)
XLA Ops:
  0.6 31.0 %layer0.1 = (bf16[8,32,256]{2,1,0:T(8,128)(2,1)S(1)}, f32[4,32,256]{2,1,0:T(8,128)S(1)}, bf16[8,64,256]{2,1,0:T(8,128)(2,1)S(1)}, bf16[8,256,1024]{2,1,0:T(8,128...) custom-call(s32[128]{0:T(128)} %len_ref.3, ...), custom_call_target="tpu_custom_call" | custom-call | tf_op jit(solution)/shard_map/layer0/pallas_call | solution.py:425
  31.6 6.9 %attend1.1 = (bf16[8,32,256]{2,1,0:T(8,128)(2,1)S(1)}, bf16[32,512,256]{2,1,0:T(8,128)(2,1)S(1)}, bf16[32,512,256]{2,1,0:T(8,128)(2,1)S(1)}, bf16[32,512,256]{2,...) custom-call(s32[128]{0:T(128)} %len_ref.3, ...), custom_call_target="tpu_custom_call", output_to_operand_aliasing={{1}: (3, {}), {2}: (4, {}), {3}: (5, {}), {4}: (6, {})} | custom-call | tf_op jit(solution)/shard_map/attend1/pallas_call | solution.py:447
  38.5 0.3 collective-permute-start
  38.8 5.9 %write1.1 = (bf16[2,32,512,256]{3,2,1,0:T(8,128)(2,1)}, bf16[2,32,512,256]{3,2,1,0:T(8,128)(2,1)}) custom-call(bf16[32,512,256]{2,1,0:T(8,128)(2,1)S(1)} %get-tuple-element.27.k1, bf16[32,512,256]{2,1,0:T(8,128)(2,1)S(1)} %get-tuple-element.28.v1, bf16[2,32,512,256]{3,2,1,0:T(8,128)(2,1)} %get-tuple-element.29._k, ...), custom_call_target="tpu_custom_call", output_to_operand_aliasing={{0}: (2, {}), {1}: (3, {})} | custom-call | flops 1000000000 | bytes 33554432 | tf_op jit(solution)/shard_map/write1/pallas_call | solution.py:460
  44.8 0.0 collective-permute-done.other
  44.8 6.8 %last.1 = bf16[128,2048]{1,0:T(8,128)(2,1)S(1)} custom-call(bf16[8,32,256]{2,1,0:T(8,128)(2,1)S(1)} %get-tuple-element.24.ctx, bf16[8,32,256]{2,1,0:T(8,128)(2,1)S(1)} %collective-permute-done.other, bf16[8,64,256]{2,1,0:T(8,128)(2,1)S(1)} %get-tuple-element.25.hid, bf16[8,256,1024]{2,1,0:T(8,128)(2,1)S(1)} %get-tuple-element.26.wof), custom_call_target="tpu_custom_call" | custom-call | tf_op jit(solution)/shard_map/last/pallas_call | solution.py:472
  51.6 0.8 %copy.24 = bf16[128,2048]{1,0:T(8,128)(2,1)} copy(bf16[128,2048]{1,0:T(8,128)(2,1)S(1)} %last.1) | data formatting | bytes 1048576
Async XLA Ops:
  38.5 6.3 %collective-permute-start = (bf16[8,32,256]{2,1,0:T(8,128)(2,1)S(1)}, bf16[8,32,256]{2,1,0:T(8,128)(2,1)S(1)}, u32[]{:S(2)}, u32[]{:S(2)}) collective-permute-start(bf16[8,32,256]{2,1,0:T(8,128)(2,1)S(1)} %get-tuple-element.24.ctx), channel_id=1, source_target_pairs={{0,3},{1,2},{2,1},{3,0},{4,7},{5,6},{6,5},{7,4},{8,11},{9,10},{10,... | collective-permute-start | bytes 393224 | tf_op jit(solution)/shard_map/ppermute | solution.py:459

commit v7 on v6

--- a/solution.py
+++ b/solution.py
@@ -40,7 +40,9 @@
         src_ref=src, dst_ref=dst, send_sem=send_sem, recv_sem=recv_sem, device_id=peer, device_id_type=MESH)
 
 
-LAG = 8
+LAG = 12
+YSTEP = 1
+HSTEP = 2
 
 
 def scatter_queries(get, qs, heads, rows):
@@ -238,10 +240,13 @@
             for i in range(1, 4):
                 y += dot(lhs[i, both, :], wos[i // 2, (i % 2) * 256:(i % 2 + 1) * 256, j * 256:(j + 1) * 256])
             ys[j, both, :] = y
-            n = g * chunks + j
-            c = send(ys.at[j, pl.ds(g * rows + half, half)], yrecv.at[j, pl.ds(g * half, half)], ysem.at[0, n], ysem.at[1, n], across)
-            c.start()
-            ycopies.append(c)
+            if j % YSTEP == YSTEP - 1:
+                n = len(ycopies)
+                part = pl.ds(j + 1 - YSTEP, YSTEP)
+                c = send(ys.at[part, pl.ds(g * rows + half, half)], yrecv.at[part, pl.ds(g * half, half)],
+                         ysem.at[0, n], ysem.at[1, n], across)
+                c.start()
+                ycopies.append(c)
     loads_kv = [[pltpu.make_async_copy(src.at[1, pl.ds(j * dim, dim)], wos.at[0, pl.ds(n * dim, dim), pl.ds(j * dim, dim)],
                                        lsem.at[4 + n, j]) for j in range(chunks)] for n, src in enumerate((wk_hbm, wv_hbm))]
     for c in loads_kv[0] + loads_kv[1]:
@@ -260,18 +265,23 @@
     hcopies = []
     for g in range(2):
         for j in range(chunks):
-            n = g * chunks + j
-            ycopies[n].wait_recv()
+            if j % YSTEP == 0:
+                ycopies[(g * chunks + j) // YSTEP].wait_recv()
             part = slice(g * half, (g + 1) * half)
             old = xs[pl.ds(pl.multiple_of(m * rows + g * half, half), half), j * 256:(j + 1) * 256]
             hl[j, part, :] = (old.astype(F32) + (ys[j, g * rows:g * rows + half, :] + yrecv[j, part, :])).astype(BF16)
-            c = send(hl.at[j, pl.ds(g * half, half)], hl.at[j, pl.ds(rows + g * half, half)], hsem.at[0, n], hsem.at[1, n], across)
-            c.start()
-            hcopies.append(c)
+            if j % HSTEP == HSTEP - 1:
+                n = len(hcopies)
+                these = pl.ds(j + 1 - HSTEP, HSTEP)
+                c = send(hl.at[these, pl.ds(g * half, half)], hl.at[these, pl.ds(rows + g * half, half)],
+                         hsem.at[0, n], hsem.at[1, n], across)
+                c.start()
+                hcopies.append(c)
     push_q1.wait()
     for j in range(chunks):
-        for g in range(2):
-            hcopies[g * chunks + j].wait_recv()
+        if j % HSTEP == 0:
+            for g in range(2):
+                hcopies[(g * chunks + j) // HSTEP].wait_recv()
         for i in range(4):
             part = dot(hl[j], wq1[i // 2, j * 256:(j + 1) * 256, (i % 2) * 256:(i % 2 + 1) * 256])
             if j == 0:

time: 52.5 us -> 52.5 us (level)
  no operation moved by 1% of the time
where the time goes in v7:
time: 52.5 us; the launch traced here: 52.4 us
  Pallas kernels  50.3 us (96%)
  local copies, waits for them, and re-layouts  0.8 us (2%)
  between operations  0.67 us (1%)
  starting transfers between devices  0.55 us (1%)
    pallas_call x1, Pallas kernels, device_step(): pl.pallas_call(layer0_kernel, out_shape=(pltpu.VMEM(hd, BF16), pltpu.VMEM...  30.8 us
    pallas_call x1, Pallas kernels, device_step(): pl.pallas_call(attend1_kernel, out_shape=(pltpu.VMEM(hd, BF16), cache, ca...  6.89 us
    pallas_call x1, Pallas kernels, device_step(): pl.pallas_call(last_kernel, out_shape=pltpu.VMEM((total, width), BF16), i...  6.69 us
    pallas_call x1, Pallas kernels, device_step(): pl.pallas_call(write1_kernel, out_shape=(jax.ShapeDtypeStruct(k_cache.sha...  5.92 us
  transfers between devices with their start and end apart: 1, of which 0 were waited for; matrix products, arithmetic and copies ran while one was open for 0% of the time, Pallas kernels for 11%

profile of v7, /device:TPU:0, one launch (start us, length us, event | category | flops | bytes accessed | tf_op | source)
XLA Modules:
  0.0 52.4 jit_solution(13889489410521700872)
XLA Ops:
  0.6 30.8 %layer0.1 = (bf16[8,32,256]{2,1,0:T(8,128)(2,1)S(1)}, f32[4,32,256]{2,1,0:T(8,128)S(1)}, bf16[8,64,256]{2,1,0:T(8,128)(2,1)S(1)}, bf16[8,256,1024]{2,1,0:T(8,128...) custom-call(s32[128]{0:T(128)} %len_ref.3, ...), custom_call_target="tpu_custom_call" | custom-call | tf_op jit(solution)/shard_map/layer0/pallas_call | solution.py:435
  31.5 6.9 %attend1.1 = (bf16[8,32,256]{2,1,0:T(8,128)(2,1)S(1)}, bf16[32,512,256]{2,1,0:T(8,128)(2,1)S(1)}, bf16[32,512,256]{2,1,0:T(8,128)(2,1)S(1)}, bf16[32,512,256]{2,...) custom-call(s32[128]{0:T(128)} %len_ref.3, ...), custom_call_target="tpu_custom_call", output_to_operand_aliasing={{1}: (3, {}), {2}: (4, {}), {3}: (5, {}), {4}: (6, {})} | custom-call | tf_op jit(solution)/shard_map/attend1/pallas_call | solution.py:457
  38.4 0.5 %collective-permute-start = (bf16[8,32,256]{2,1,0:T(8,128)(2,1)S(1)}, bf16[8,32,256]{2,1,0:T(8,128)(2,1)S(1)}, u32[]{:S(2)}, u32[]{:S(2)}) collective-permute-start(bf16[8,32,256]{2,1,0:T(8,128)(2,1)S(1)} %get-tuple-element.24.ctx), channel_id=1, source_target_pairs={{0,3},{1,2},{2,1},{3,0},{4,7},{5,6},{6,5},{7,4},{8,11},{9,10},{10,... | collective-permute-start | bytes 393224 | tf_op jit(solution)/shard_map/ppermute | solution.py:469
  38.9 5.9 %write1.1 = (bf16[2,32,512,256]{3,2,1,0:T(8,128)(2,1)}, bf16[2,32,512,256]{3,2,1,0:T(8,128)(2,1)}) custom-call(bf16[32,512,256]{2,1,0:T(8,128)(2,1)S(1)} %get-tuple-element.27.k1, bf16[32,512,256]{2,1,0:T(8,128)(2,1)S(1)} %get-tuple-element.28.v1, bf16[2,32,512,256]{3,2,1,0:T(8,128)(2,1)} %get-tuple-element.29._k, ...), custom_call_target="tpu_custom_call", output_to_operand_aliasing={{0}: (2, {}), {1}: (3, {})} | custom-call | flops 1000000000 | bytes 33554432 | tf_op jit(solution)/shard_map/write1/pallas_call | solution.py:470
  44.8 0.0 collective-permute-done.other
  44.9 6.7 %last.1 = bf16[128,2048]{1,0:T(8,128)(2,1)S(1)} custom-call(bf16[8,32,256]{2,1,0:T(8,128)(2,1)S(1)} %get-tuple-element.24.ctx, bf16[8,32,256]{2,1,0:T(8,128)(2,1)S(1)} %collective-permute-done.other, bf16[8,64,256]{2,1,0:T(8,128)(2,1)S(1)} %get-tuple-element.25.hid, bf16[8,256,1024]{2,1,0:T(8,128)(2,1)S(1)} %get-tuple-element.26.wof), custom_call_target="tpu_custom_call" | custom-call | tf_op jit(solution)/shard_map/last/pallas_call | solution.py:482
  51.6 0.8 %copy.24 = bf16[128,2048]{1,0:T(8,128)(2,1)} copy(bf16[128,2048]{1,0:T(8,128)(2,1)S(1)} %last.1) | data formatting | bytes 1048576
Async XLA Ops:
  38.4 6.5 %collective-permute-start = (bf16[8,32,256]{2,1,0:T(8,128)(2,1)S(1)}, bf16[8,32,256]{2,1,0:T(8,128)(2,1)S(1)}, u32[]{:S(2)}, u32[]{:S(2)}) collective-permute-start(bf16[8,32,256]{2,1,0:T(8,128)(2,1)S(1)} %get-tuple-element.24.ctx), channel_id=1, source_target_pairs={{0,3},{1,2},{2,1},{3,0},{4,7},{5,6},{6,5},{7,4},{8,11},{9,10},{10,... | collective-permute-start | bytes 393224 | tf_op jit(solution)/shard_map/ppermute | solution.py:469
